TPU v7x, 128 devices: a whole 4x4x4 slice. The times are simulated.
128 devices in a mesh: dp: 1, tp: 2 (over core), sp: 64 (over z, y, x).
Axes of the slice: x: 4, y: 4, z: 4, core: 2. Of those that a mesh axis runs over, the one named last changes fastest.
Arguments:
- hidden: bfloat16 [32, 6144], P('dp')
- norm_w: bfloat16 [6144], replicated
- w_q: bfloat16 [6144, 6144], P(None, 'tp')
- b_q: bfloat16 [6144], P('tp')
- w_k: bfloat16 [6144, 256], P(None, 'tp')
- b_k: bfloat16 [256], P('tp')
- w_v: bfloat16 [6144, 256], P(None, 'tp')
- b_v: bfloat16 [256], P('tp')
- w_o: bfloat16 [6144, 6144], P('tp')
- k_cache: bfloat16 [32, 32768, 2, 128], P('dp', 'sp', 'tp')
- v_cache: bfloat16 [32, 32768, 2, 128], P('dp', 'sp', 'tp')
- positions: int32 [32], P('dp')
- seq_lens: int32 [32], P('dp')
Outputs:
- output 1: bfloat16 [32, 6144], P('dp')
- output 2: bfloat16 [32, 2, 128], P('dp', 'tp')
- output 3: bfloat16 [32, 2, 128], P('dp', 'tp')
All inputs are finite; a program needn't handle non-finite values.
Results may differ from a plain program's by a relative error of at most 0.00881808.
Values sent between devices are 32-bit elements.
A program may use at most 1 GiB of HBM per device.

v0:
```python
import jax
import jax.numpy as jnp
from jax import lax
from jax.sharding import PartitionSpec as P

RMS_EPS = 1.5625e-7
ROPE_BASE = 10000.0
NEG_BIG = -1e30


def rms_norm(x_rows, norm_w):
    x_f32 = x_rows.astype(jnp.float32)
    mean_sq = jnp.mean(x_f32 * x_f32, axis=-1, keepdims=True)
    return (x_f32 * lax.rsqrt(mean_sq + RMS_EPS) * norm_w.astype(jnp.float32)).astype(jnp.bfloat16)


def apply_rotary(heads_in, positions):
    rot_dim = heads_in.shape[-1] // 2
    half_rot = rot_dim // 2
    inv_freq = ROPE_BASE ** (-2.0 * jnp.arange(half_rot, dtype=jnp.float32) / rot_dim)
    angles = positions.astype(jnp.float32)[:, None, None] * inv_freq
    cos_t = jnp.cos(angles)
    sin_t = jnp.sin(angles)
    rot_pairs = heads_in[..., :rot_dim].astype(jnp.float32).reshape(heads_in.shape[:-1] + (half_rot, 2))
    even_part = rot_pairs[..., 0]
    odd_part = rot_pairs[..., 1]
    rotated = jnp.stack([even_part * cos_t - odd_part * sin_t, even_part * sin_t + odd_part * cos_t], axis=-1)
    rotated = rotated.reshape(heads_in.shape[:-1] + (rot_dim,)).astype(jnp.bfloat16)
    return jnp.concatenate([rotated, heads_in[..., rot_dim:]], axis=-1)


def project(normed, weight, bias_vec):
    return (jnp.dot(normed, weight, preferred_element_type=jnp.float32) + bias_vec.astype(jnp.float32)).astype(jnp.bfloat16)


def local_partials(q_grp, k_rot, v_new, k_loc, v_loc, seq_lens, shard_idx):
    s_dev = k_loc.shape[1]
    attn_scale = q_grp.shape[-1] ** -0.5
    cache_pos = shard_idx * s_dev + jnp.arange(s_dev, dtype=jnp.int32)
    valid_mask = (cache_pos[None, :] < seq_lens[:, None])[:, None, None, :]
    s_cache = jnp.einsum('bgqd,bsgd->bgqs', q_grp, k_loc, preferred_element_type=jnp.float32) * attn_scale
    s_cache = jnp.where(valid_mask, s_cache, NEG_BIG)
    is_first = shard_idx == 0
    s_new = jnp.einsum('bgqd,bgd->bgq', q_grp, k_rot, preferred_element_type=jnp.float32) * attn_scale
    s_new = jnp.where(is_first, s_new, NEG_BIG)
    m_loc = jnp.maximum(jnp.max(s_cache, axis=-1), s_new)
    p_cache = jnp.where(valid_mask, jnp.exp(s_cache - m_loc[..., None]), 0.0)
    p_new = jnp.where(is_first, jnp.exp(s_new - m_loc), 0.0)
    l_loc = jnp.sum(p_cache, axis=-1) + p_new
    o_loc = jnp.einsum('bgqs,bsgd->bgqd', p_cache.astype(jnp.bfloat16), v_loc, preferred_element_type=jnp.float32)
    o_loc = o_loc + p_new[..., None] * v_new.astype(jnp.float32)[:, :, None, :]
    return m_loc, l_loc, o_loc


def solution(mesh):
    def device_step(hidden, norm_w, w_q, b_q, w_k, b_k, w_v, b_v, w_o, k_cache, v_cache, positions, seq_lens):
        n_rows = hidden.shape[0]
        groups_dev, head_dim = k_cache.shape[2], k_cache.shape[3]
        heads_dev = w_q.shape[1] // head_dim
        per_group = heads_dev // groups_dev
        normed = rms_norm(hidden, norm_w)
        q_rot = apply_rotary(project(normed, w_q, b_q).reshape(n_rows, heads_dev, head_dim), positions)
        k_rot = apply_rotary(project(normed, w_k, b_k).reshape(n_rows, groups_dev, head_dim), positions)
        v_new = project(normed, w_v, b_v).reshape(n_rows, groups_dev, head_dim)
        q_grp = q_rot.reshape(n_rows, groups_dev, per_group, head_dim)
        m_loc, l_loc, o_loc = local_partials(q_grp, k_rot, v_new, k_cache, v_cache, seq_lens, lax.axis_index('sp'))
        m_all = lax.pmax(m_loc, 'sp')
        factor = jnp.exp(m_loc - m_all)
        l_all, o_all = lax.psum((l_loc * factor, o_loc * factor[..., None]), 'sp')
        attn_rows = (o_all / l_all[..., None]).astype(jnp.bfloat16).reshape(n_rows, heads_dev * head_dim)
        proj_sum = lax.psum(jnp.dot(attn_rows, w_o, preferred_element_type=jnp.float32), 'tp')
        y_out = (hidden.astype(jnp.float32) + proj_sum).astype(jnp.bfloat16)
        return y_out, k_rot, v_new

    col_spec = P(None, 'tp')
    vec_spec = P('tp')
    cache_spec = P('dp', 'sp', 'tp', None)
    group_spec = P('dp', 'tp', None)
    in_specs = (P('dp', None), P(None), col_spec, vec_spec, col_spec, vec_spec, col_spec, vec_spec,
                P('tp', None), cache_spec, cache_spec, P('dp'), P('dp'))
    out_specs = (P('dp', None), group_spec, group_spec)
    return jax.shard_map(device_step, mesh=mesh, in_specs=in_specs, out_specs=out_specs, check_vma=False)
```

profile of v0, /device:TPU:1, one launch (start us, length us, event | category | flops | bytes accessed | tf_op | source)
XLA Modules:
  0.0 780.7 jit_solution(459563374084458623)
XLA Ops:
  7.2 0.0 copy-start
  7.2 0.0 all-reduce.3.cloned.1.call-start
  7.3 0.8 convert_element_type.69
  8.1 0.7 convert_element_type.71
  8.7 1.2 convert_element_type.75
  9.9 1.2 fusion.22
  11.1 0.7 convert_element_type.67
  11.8 0.7 convert_element_type.65
  12.5 1.9 fusion.21
  14.5 0.1 slice_convert_fusion.1
  14.5 0.1 copy.22
  14.7 0.1 copy.30
  14.7 0.1 copy.29
  14.8 0.1 multiply_cosine_fusion.1
  15.0 0.1 fusion.39
  15.1 0.1 copy.25
  15.2 0.1 copy.26
  15.3 0.0 copy-start.11
  15.3 15.2 %fusion.18 = bf16[4,8,24,128]{3,1,2,0:T(8,128)(2,1)S(1)} fusion(bf16[6144,3072]{1,0:T(8,128)(2,1)} %param.15, f32[3072]{0:T(1024)S(1)} %convert_element_type.67, bf16[32,6144]{1,0:T(8,128)(2,1)S(1)} %copy-done.2, f32[6144]{0:T(1024)S(1)} %convert_element_type.65, f32[32]{0:T(128)S(1)} %add_rsqrt_fusion), kind=kOutput, calls=%fused_computation.16 | convolution fusion | flops 1208942592 | bytes 38375552 | tf_op jit(solution)/shard_map/dot_general | solution.py:33
  30.6 0.1 slice_convert_fusion
  30.7 0.0 copy-start.4
  30.7 0.3 copy.20
  31.1 0.0 copy-start.19
  31.1 0.1 subtract_convert_fusion
  31.2 0.1 pad_maximum_fusion
  31.3 0.3 copy.21
  31.6 0.1 copy-done.19
  31.7 0.1 broadcast_compare_fusion
  31.9 0.1 fusion.59
  31.9 0.5 copy-done.3
  32.4 0.3 fusion.33
  32.7 4.8 fusion.53
  37.5 0.0 copy-done.13
  37.5 296.4 %pmax.7 = f32[32,1,24]{2,0,1:T(8,128)} all-reduce(f32[32,1,24]{2,0,1:T(8,128)S(1)} %bitcast.58), channel_id=1, replica_groups=mesh['dp'=1,'tp'=2,'sp'=64] {'sp'}, use_global_device_ids=true, to_apply=%region_2.3 | all-reduce | flops 768 | bytes 6144 | tf_op jit(solution)/shard_map/pmax | solution.py:67
  333.9 0.0 copy-start.15
  333.9 1.3 fusion.7
  335.3 1.0 fusion.54
  336.3 3.8 fusion.15
  340.1 0.0 all-reduce.3.cloned.1.call-update
  340.2 0.0 all-reduce.5.cloned.1.call-start
  340.2 286.2 %psum.22 = f32[32,24]{1,0:T(8,128)S(1)} all-reduce(f32[32,24]{1,0:T(8,128)S(1)} %get-tuple-element.3), channel_id=1, replica_groups=mesh['dp'=1,'tp'=2,'sp'=64] {'sp'}, use_global_device_ids=true, to_apply=%region_5.6 | all-reduce | flops 768 | bytes 6144 | tf_op jit(solution)/shard_map/psum | solution.py:69
  626.4 1.2 divide_convert_fusion
  627.6 0.0 copy-start.10
  627.6 16.1 %fusion.30 = f32[32,6144]{1,0:T(8,128)} fusion(bf16[3072,6144]{1,0:T(8,128)(2,1)} %param.21, bf16[4,8,24,128]{3,2,1,0:T(8,128)(2,1)S(1)} %bitcast.57), kind=kOutput, calls=%fused_computation.33 | convolution fusion | flops 1207959552 | bytes 38731776 | tf_op jit(solution)/shard_map/dot_general | solution.py:71
  643.8 0.0 all-reduce.5.cloned.1.call-update
  643.8 0.7 pad_maximum_fusion.5
  644.5 127.4 %all-reduce.5.cloned.1.call-done = f32[32,6144]{1,0:T(8,128)} async-done(((f32[32,6144]{1,0:T(8,128)}), f32[32,6144]{1,0:T(8,128)}) %all-reduce.5.cloned.1.call-update) | async-done | bytes 786448 | tf_op jit(solution)/shard_map/psum | solution.py:71
  771.9 1.9 fusion.25
  (40 shorter events, 0.2 us)
Async XLA Ops:
  7.2 328.1 %copy-start = (bf16[6144,128]{1,0:T(8,128)(2,1)S(1)}, bf16[6144,128]{1,0:T(8,128)(2,1)}, u32[]{:S(2)}) copy-start(bf16[6144,128]{1,0:T(8,128)(2,1)} %param.19) | copy-start | bytes 4718596
  7.2 8.1 %copy-start.2 = (bf16[32,6144]{1,0:T(8,128)(2,1)S(1)}, bf16[32,6144]{1,0:T(8,128)(2,1)}, u32[]{:S(2)}) copy-start(bf16[32,6144]{1,0:T(8,128)(2,1)} %param.13) | copy-start | bytes 1179652
  7.2 619.2 %all-reduce.3.cloned.1.call-start = ((), (), s32[]{:S(2)}) async-start(), calls=%async_computation | async-start | bytes 786432 | tf_op jit(solution)/shard_map/psum | solution.py:69
  11.1 19.5 %copy-start.16 = (f32[32]{0:T(128)}, f32[32]{0:T(128)S(1)}, u32[]{:S(2)}) copy-start(f32[32]{0:T(128)S(1)} %add_rsqrt_fusion) | copy-start | bytes 388
  12.5 18.0 %copy-start.5 = (f32[6144]{0:T(1024)}, f32[6144]{0:T(1024)S(1)}, u32[]{:S(2)}) copy-start(f32[6144]{0:T(1024)S(1)} %convert_element_type.65) | copy-start | bytes 73732
  14.5 17.3 %copy-start.9 = (bf16[32,1,64]{2,0,1:T(8,128)(2,1)}, bf16[32,1,64]{2,0,1:T(8,128)(2,1)S(1)}, u32[]{:S(2)}) copy-start(bf16[32,1,64]{2,0,1:T(8,128)(2,1)S(1)} %get-tuple-element.15) | copy-start | bytes 12292
  15.3 16.5 %copy-start.11 = (bf16[32,1,64]{2,0,1:T(8,128)(2,1)}, bf16[32,1,64]{2,0,1:T(8,128)(2,1)S(1)}, u32[]{:S(2)}) copy-start(bf16[32,1,64]{2,0,1:T(8,128)(2,1)S(1)} %copy.26) | copy-start | bytes 12292
  30.7 1.2 copy-start.4
  31.1 0.7 copy-start.19
  31.7 0.7 copy-start.3
  31.8 5.7 copy-start.7
  32.7 4.8 copy-start.13
  333.9 1.3 copy-start.6
  333.9 1.4 copy-start.17
  333.9 1.4 copy-start.18
  333.9 2.4 copy-start.14
  333.9 2.4 copy-start.15
  333.9 2.4 copy-start.8
  340.2 431.7 %all-reduce.5.cloned.1.call-start = ((), (), s32[]{:S(2)}) async-start(), calls=%async_computation.1 | async-start | bytes 1572864 | tf_op jit(solution)/shard_map/psum | solution.py:71
  627.6 16.2 %copy-start.10 = (bf16[32,1,64]{2,0,1:T(8,128)(2,1)S(1)}, bf16[32,1,64]{2,0,1:T(8,128)(2,1)}, u32[]{:S(2)}) copy-start(bf16[32,1,64]{2,0,1:T(8,128)(2,1)} %copy-done.9) | copy-start | bytes 12292
  627.6 16.2 %copy-start.12 = (bf16[32,1,64]{2,0,1:T(8,128)(2,1)S(1)}, bf16[32,1,64]{2,0,1:T(8,128)(2,1)}, u32[]{:S(2)}) copy-start(bf16[32,1,64]{2,0,1:T(8,128)(2,1)} %copy-done.11) | copy-start | bytes 12292
  627.6 146.2 %copy-start.1 = (bf16[6144,128]{1,0:T(8,128)(2,1)S(1)}, bf16[6144,128]{1,0:T(8,128)(2,1)}, u32[]{:S(2)}) copy-start(bf16[6144,128]{1,0:T(8,128)(2,1)} %param.19) | copy-start | bytes 4718596
Sparse Core Ops, SparseCore 0:
  340.3 174.9 all-reduce.2
  643.9 127.9 all-reduce.4
where the time goes:
time: 781 us
  blocking collectives  583 us (75%)
  waiting for transfers between devices  127 us (16%)
  matrix products  43.2 us (6%)
  between operations  14.4 us (2%)
  other arithmetic  11.2 us (1%)
    pmax x1, blocking collectives, device_step(): m_all = lax.pmax(m_loc, 'sp')  296 us
    psum x1, blocking collectives, device_step(): l_all, o_all = lax.psum((l_loc * factor, o_loc * factor[..., None]), 'sp')  286 us
    psum x1, waiting for transfers between devices, device_step(): lax.psum(jnp.dot(attn_rows, w_o, preferred_element_type=jnp.float32), 'tp')  127 us
    dot_general x3, matrix products, project(): jnp.dot(normed, weight, preferred_element_type=jnp.float32)  18.2 us
    dot_general x1, matrix products, device_step(): jnp.dot(attn_rows, w_o, preferred_element_type=jnp.float32)  16.1 us
  transfers between devices with their start and end apart: 2, of which 1 were waited for; matrix products, arithmetic and copies ran while one was open for 0% of the time, Pallas kernels for 0%

commit v1 on v0

v1 whole, which is shorter than its diff:
```python
import functools
import math

import jax
import jax.numpy as jnp
from jax import lax
from jax.experimental import pallas as pl
from jax.experimental.pallas import tpu as pltpu
from jax.sharding import PartitionSpec as P

RMS_EPS = 1.5625e-7
ROPE_BASE = 10000.0
NEG_BIG = -3.0e38
MESH = pl.DeviceIdType.MESH
F32 = jnp.float32
BF16 = jnp.bfloat16

N_ROWS = 32
S_DEV = 512
D = 128
SP = 64
PLANE = 16
HALF = 12
SLOT = 16
N_OUT = 6144
N_Z = 1536
AG = 24
UNROLL = 4


def rms_norm(x_rows, norm_w):
    x_f32 = x_rows.astype(jnp.float32)
    mean_sq = jnp.mean(x_f32 * x_f32, axis=-1, keepdims=True)
    return (x_f32 * lax.rsqrt(mean_sq + RMS_EPS) * norm_w.astype(jnp.float32)).astype(jnp.bfloat16)


def apply_rotary(heads_in, positions):
    rot_dim = heads_in.shape[-1] // 2
    half_rot = rot_dim // 2
    inv_freq = ROPE_BASE ** (-2.0 * jnp.arange(half_rot, dtype=jnp.float32) / rot_dim)
    angles = positions.astype(jnp.float32)[:, None, None] * inv_freq
    cos_t = jnp.cos(angles)
    sin_t = jnp.sin(angles)
    rot_pairs = heads_in[..., :rot_dim].astype(jnp.float32).reshape(heads_in.shape[:-1] + (half_rot, 2))
    even_part = rot_pairs[..., 0]
    odd_part = rot_pairs[..., 1]
    rotated = jnp.stack([even_part * cos_t - odd_part * sin_t, even_part * sin_t + odd_part * cos_t], axis=-1)
    rotated = rotated.reshape(heads_in.shape[:-1] + (rot_dim,)).astype(jnp.bfloat16)
    return jnp.concatenate([rotated, heads_in[..., rot_dim:]], axis=-1)


def project(normed, weight, bias_vec):
    return (jnp.dot(normed, weight, preferred_element_type=jnp.float32) + bias_vec.astype(jnp.float32)).astype(jnp.bfloat16)


def tail_kernel(q_ref, kn_ref, vn_ref, seq_ref, hid_ref, k_hbm, v_hbm, wo_hbm, y_ref,
                kbuf, vbuf, wobuf, o_send, o_recv, a_all, lhs, ypart, yrecv, ag,
                ksem, vsem, wsem, rs_send, rs_recv, z_send, z_recv, d_send, d_recv,
                ag_send, ag_recv, f_send, f_recv):
    c = lax.axis_index('tp')
    s = lax.axis_index('sp')
    z = lax.div(s, PLANE)
    p = lax.rem(s, PLANE)
    qk_scale = (D ** -0.5) * math.log2(math.e)

    def chip_of(i):
        return lax.rem(p + 1 + lax.div(i, 2), PLANE)

    def row_of(i):
        return chip_of(i) + PLANE * lax.rem(i, 2)

    barrier = pltpu.get_barrier_semaphore()

    def greet(d, carry):
        pl.semaphore_signal(barrier, inc=1, device_id={'sp': lax.rem(s + d, SP)}, device_id_type=MESH)
        return carry
    lax.fori_loop(1, SP, greet, 0)
    pl.semaphore_signal(barrier, inc=1, device_id={'tp': 1 - c}, device_id_type=MESH)

    def k_copy(i):
        return pltpu.make_async_copy(k_hbm.at[row_of(i)], kbuf.at[i], ksem.at[i])

    def v_copy(i):
        return pltpu.make_async_copy(v_hbm.at[row_of(i)], vbuf.at[i], vsem.at[i])

    def start_kv(i, carry):
        k_copy(i).start()
        v_copy(i).start()
        return carry
    lax.fori_loop(0, N_ROWS, start_kv, 0)
    wo_copies = [pltpu.make_async_copy(
        wo_hbm.at[pl.ds(768 * j, 768), pl.ds(pl.multiple_of(z * N_Z, N_Z), N_Z)],
        wobuf.at[pl.ds(768 * j, 768)], wsem.at[j]) for j in range(4)]
    for cp in wo_copies:
        cp.start()

    pl.semaphore_wait(barrier, SP)

    lane = lax.broadcasted_iota(jnp.int32, (SLOT, D), 1)
    sub = lax.broadcasted_iota(jnp.int32, (SLOT, D), 0)
    eye = lane == sub
    pos = s * S_DEV + lax.broadcasted_iota(jnp.int32, (2 * SLOT, S_DEV), 1)

    def rs_copy(i, hf):
        dest = (2 * lax.rem(i, 2) + hf) * PLANE + chip_of(i)
        slot = 2 * i + hf
        return dest, pltpu.make_async_remote_copy(
            src_ref=o_send.at[slot], dst_ref=o_recv.at[pl.ds(pl.multiple_of(s * SLOT, SLOT), SLOT)],
            send_sem=rs_send, recv_sem=rs_recv, device_id={'sp': dest}, device_id_type=MESH)

    def rows_step(g, carry):
        idx = [g * UNROLL + u for u in range(UNROLL)]
        rows = [row_of(i) for i in idx]
        scores = []
        for i, b in zip(idx, rows):
            k_copy(i).wait()
            sc = lax.dot_general(q_ref[b], kbuf[i], (((1,), (1,)), ((), ())), preferred_element_type=F32)
            scores.append(jnp.where(pos < seq_ref[b], sc, NEG_BIG))
        tops = [jnp.max(sc, axis=1, keepdims=True) for sc in scores]
        probs = [jnp.exp2((sc - m) * qk_scale) for sc, m in zip(scores, tops)]
        sums = [jnp.sum(pr, axis=1, keepdims=True) for pr in probs]
        for i, m, l, pr in zip(idx, tops, sums, probs):
            v_copy(i).wait()
            o = jnp.dot(pr.astype(BF16), vbuf[i], preferred_element_type=F32)
            m2 = m * qk_scale
            for hf in range(2):
                part = slice(hf * SLOT, (hf + 1) * SLOT)
                m_row = jnp.sum(jnp.where(eye, m2[part], 0.0), axis=0, keepdims=True)
                l_row = jnp.sum(jnp.where(eye, l[part], 0.0), axis=0, keepdims=True)
                o_send[2 * i + hf] = jnp.where(sub == HALF, m_row, jnp.where(sub == HALF + 1, l_row, o[part]))
        for i in idx:
            for hf in range(2):
                dest, cp = rs_copy(i, hf)

                @pl.when(dest != s)
                def _():
                    cp.start()

                @pl.when(dest == s)
                def _():
                    o_recv[pl.ds(pl.multiple_of(s * SLOT, SLOT), SLOT), :] = o_send[2 * i + hf]
        return carry
    lax.fori_loop(0, N_ROWS // UNROLL, rows_step, 0)

    my_row = p + PLANE * lax.div(z, 2)
    my_half = lax.rem(z, 2)
    q_mine = q_ref[my_row, pl.ds(pl.multiple_of(my_half * SLOT, SLOT), SLOT), :].astype(F32)
    k_mine = kn_ref[my_row]
    v_mine = vn_ref[my_row]
    s_new = jnp.sum(q_mine * k_mine, axis=1, keepdims=True) * qk_scale

    def all_in(ref, sem):
        pltpu.make_async_copy(ref, ref, sem).wait()

    all_in(o_recv.at[pl.ds(0, (SP - 1) * SLOT)], rs_recv)
    m_rows = o_recv[pl.ds(HALF, SP, stride=SLOT), :]
    l_rows = o_recv[pl.ds(HALF + 1, SP, stride=SLOT), :]
    stats = jnp.transpose(jnp.concatenate([m_rows, l_rows], axis=0))[:SLOT]
    m_cols, l_cols = stats[:, :SP], stats[:, SP:]
    m_top = jnp.maximum(jnp.max(m_cols, axis=1, keepdims=True), s_new)
    w_cols = jnp.exp2(m_cols - m_top)
    w_new = jnp.exp2(s_new - m_top)
    l_all = jnp.sum(w_cols * l_cols, axis=1, keepdims=True) + w_new
    acc = w_new * v_mine
    for j in range(SP):
        acc = acc + w_cols[:, j:j + 1] * o_recv[j * SLOT:(j + 1) * SLOT, :]
    a_all[z] = acc / l_all

    z_copies = []
    for dz in range(1, 4):
        z_copies.append(pltpu.make_async_remote_copy(
            src_ref=a_all.at[z], dst_ref=a_all.at[z], send_sem=z_send.at[dz - 1], recv_sem=z_recv.at[dz - 1],
            device_id={'sp': lax.rem(z + dz, 4) * PLANE + p}, device_id_type=MESH))
    for cp in z_copies:
        cp.start()
    lhs[...] = jnp.zeros_like(lhs)
    for cp in z_copies:
        cp.wait_recv()
    for zz in range(4):
        r, hf = zz // 2, zz % 2
        for j in range(HALF):
            lhs[r:r + 1, (hf * HALF + j) * D:(hf * HALF + j + 1) * D] = a_all[zz, j:j + 1, :]
    for cp in wo_copies:
        cp.wait()
    ypart[0] = jnp.dot(lhs[...].astype(BF16), wobuf[...], preferred_element_type=F32)

    d_copy = pltpu.make_async_remote_copy(
        src_ref=ypart.at[0], dst_ref=ypart.at[1], send_sem=d_send, recv_sem=d_recv,
        device_id={'tp': 1 - c}, device_id_type=MESH)
    d_copy.start()
    d_copy.wait_recv()
    both = ypart[0] + ypart[1]

    def ag_slot(i):
        return ag.at[pl.ds(pl.multiple_of(i * AG, 8), AG)]

    for r in range(2):
        for blk in range(12):
            yrecv[r * 12 + blk:r * 12 + blk + 1, :] = both[r:r + 1, blk * D:(blk + 1) * D]
    ag[pl.ds(pl.multiple_of(s * AG, 8), AG), :] = yrecv[...]
    par = lax.rem(s + c, 2)

    def ag_copy(i):
        dest = 2 * i + par
        return dest, pltpu.make_async_remote_copy(
            src_ref=ag_slot(s), dst_ref=ag_slot(s), send_sem=ag_send.at[i], recv_sem=ag_recv.at[lax.div(s, 2)],
            device_id={'sp': dest}, device_id_type=MESH)

    def ag_start(i, carry):
        dest, cp = ag_copy(i)

        @pl.when(dest != s)
        def _():
            cp.start()
        return carry
    lax.fori_loop(0, SP // 2, ag_start, 0)

    def forward(i):
        return pltpu.make_async_remote_copy(
            src_ref=ag_slot(2 * i + par), dst_ref=ag_slot(2 * i + par), send_sem=f_send.at[i], recv_sem=f_recv.at[i],
            device_id={'tp': 1 - c}, device_id_type=MESH)

    def relay(i, carry):
        src = 2 * i + par

        @pl.when(src != s)
        def _():
            pltpu.make_async_copy(ag_slot(src), ag_slot(src), ag_recv.at[i]).wait()
            forward(i).start()
        return carry
    lax.fori_loop(0, SP // 2, relay, 0)

    def relayed(i, carry):
        src = 2 * i + 1 - par

        @pl.when(src != s)
        def _():
            pltpu.make_async_copy(ag_slot(src), ag_slot(src), f_recv.at[i]).wait()
        return carry
    lax.fori_loop(0, SP // 2, relayed, 0)

    for zz in range(4):
        for blk in range(12):
            col = slice(zz * N_Z + blk * D, zz * N_Z + (blk + 1) * D)
            for r in range(2):
                rows = slice(PLANE * r, PLANE * (r + 1))
                y_blk = ag[pl.ds(zz * PLANE * AG + r * 12 + blk, PLANE, stride=AG), :]
                y_ref[rows, col] = (hid_ref[rows, col].astype(F32) + y_blk).astype(BF16)

    all_in(o_send.at[pl.ds(0, SP - 1)], rs_send)
    for cp in z_copies:
        cp.wait_send()
    d_copy.wait_send()

    def drain(i, carry):
        dest, cp = ag_copy(i)

        @pl.when(dest != s)
        def _():
            cp.wait_send()

        @pl.when(2 * i + par != s)
        def _():
            forward(i).wait_send()
        return carry
    lax.fori_loop(0, SP // 2, drain, 0)


def tail(q_pad, k_new, v_new, seq_lens, hidden, k_cache, v_cache, w_o):
    vmem = pl.BlockSpec(memory_space=pltpu.VMEM)
    hbm = pl.BlockSpec(memory_space=pl.ANY)
    dma = pltpu.SemaphoreType.DMA
    return pl.pallas_call(
        tail_kernel,
        out_shape=jax.ShapeDtypeStruct((N_ROWS, N_OUT), BF16),
        in_specs=[vmem, vmem, vmem, pl.BlockSpec(memory_space=pltpu.SMEM), vmem, hbm, hbm, hbm],
        out_specs=vmem,
        scratch_shapes=[
            pltpu.VMEM((N_ROWS, S_DEV, D), BF16),
            pltpu.VMEM((N_ROWS, S_DEV, D), BF16),
            pltpu.VMEM((3072, N_Z), BF16),
            pltpu.VMEM((2 * N_ROWS, SLOT, D), F32),
            pltpu.VMEM((SP * SLOT, D), F32),
            pltpu.VMEM((4, SLOT, D), F32),
            pltpu.VMEM((8, 3072), F32),
            pltpu.VMEM((2, 8, N_Z), F32),
            pltpu.VMEM((AG, D), F32),
            pltpu.VMEM((SP * AG, D), F32),
            dma((N_ROWS,)), dma((N_ROWS,)), dma((4,)),
            dma, dma, dma((3,)), dma((3,)), dma, dma,
            dma((SP // 2,)), dma((SP // 2,)), dma((SP // 2,)), dma((SP // 2,)),
        ],
        compiler_params=pltpu.CompilerParams(
            collective_id=0, has_side_effects=True, vmem_limit_bytes=48 * 1024 * 1024),
        name='tail',
    )(q_pad, k_new, v_new, seq_lens, hidden, k_cache, v_cache, w_o)


def solution(mesh):
    def device_step(hidden, norm_w, w_q, b_q, w_k, b_k, w_v, b_v, w_o, k_cache, v_cache, positions, seq_lens):
        n_rows = hidden.shape[0]
        normed = rms_norm(hidden, norm_w)
        q_rot = apply_rotary(project(normed, w_q, b_q).reshape(n_rows, 24, D), positions)
        k_rot = apply_rotary(project(normed, w_k, b_k).reshape(n_rows, 1, D), positions)
        v_new = project(normed, w_v, b_v).reshape(n_rows, 1, D)
        q_pad = jnp.pad(q_rot.reshape(n_rows, 2, HALF, D), ((0, 0), (0, 0), (0, SLOT - HALF), (0, 0)))
        q_pad = q_pad.reshape(n_rows, 2 * SLOT, D)
        y_out = tail(q_pad, k_rot.astype(F32), v_new.astype(F32), seq_lens, hidden,
                     k_cache.reshape(n_rows, S_DEV, D), v_cache.reshape(n_rows, S_DEV, D), w_o)
        return y_out, k_rot, v_new

    col_spec = P(None, 'tp')
    vec_spec = P('tp')
    cache_spec = P('dp', 'sp', 'tp', None)
    group_spec = P('dp', 'tp', None)
    in_specs = (P('dp', None), P(None), col_spec, vec_spec, col_spec, vec_spec, col_spec, vec_spec,
                P('tp', None), cache_spec, cache_spec, P('dp'), P('dp'))
    out_specs = (P('dp', None), group_spec, group_spec)
    return jax.shard_map(device_step, mesh=mesh, in_specs=in_specs, out_specs=out_specs, check_vma=False)
```

time: 781 us -> 73.9 us (0.09)
  blocking collectives: 583 us -> 0 us
  waiting for transfers between devices: 127 us -> 0 us
  Pallas kernels: 0 us -> 43.7 us
  matrix products: 43.2 us -> 18.2 us
  between operations: 14.4 us -> 0.83 us
    pmax x1 -> x0, blocking collectives: 296 us -> none  [device_step(): m_all = lax.pmax(m_loc, 'sp')]
    psum x1 -> x0, blocking collectives: 286 us -> none  [device_step(): l_all, o_all = lax.psum((l_loc * factor, o_loc * factor[..., None]), 'sp')]
    psum x2 -> x0, waiting for transfers between devices: 127 us -> none  [the longest x1 127 us: device_step(): lax.psum(jnp.dot(attn_rows, w_o, preferred_element_type=jnp.float32), 'tp')]
    pallas_call x0 -> x1, Pallas kernels: none -> 43.7 us  [tail(): pl.pallas_call(tail_kernel, out_shape=jax.ShapeDtypeStruct((N_ROWS, N_OUT...]
    dot_general x4 -> x0, matrix products: 25 us -> none  [the longest x1 16.1 us: device_step(): jnp.dot(attn_rows, w_o, preferred_element_type=jnp.float32)]
  transfers between devices with their start and end apart: 2 -> 0, of which waited for: 1 -> 0; matrix products, arithmetic and copies ran while one was open for 0% -> 0% of each run, Pallas kernels for 0% -> 0%
where the time goes in v1:
time: 73.9 us; the launch traced here: 73.6 us
  Pallas kernels  43.7 us (59%)
  matrix products  18.2 us (25%)
  other arithmetic  5.62 us (8%)
  local copies, waits for them, and re-layouts  5.32 us (7%)
  between operations  0.83 us (1%)
    pallas_call x1, Pallas kernels, tail(): pl.pallas_call(tail_kernel, out_shape=jax.ShapeDtypeStruct((N_ROWS, N_OUT...  43.7 us
    dot_general x3, matrix products, project(): jnp.dot(normed, weight, preferred_element_type=jnp.float32)  18.2 us
    unnamed x19, local copies, waits for them, and re-layouts  4.39 us
    convert_element_type x3, other arithmetic, project(): bias_vec.astype(jnp.float32)  2.02 us

profile of v1, /device:TPU:1, one launch (start us, length us, event | category | flops | bytes accessed | tf_op | source)
XLA Modules:
  0.0 73.6 jit_solution(17892240661352183382)
XLA Ops:
  0.6 0.0 copy-start
  0.6 0.0 copy-start.2
  0.7 0.8 %convert_element_type.72 = f32[32]{0:T(128)S(1)} convert(s32[32]{0:T(128)} %param.24) | non-fusion elementwise | flops 32 | bytes 256 | tf_op jit(solution)/shard_map/convert_element_type | solution.py:41
  1.5 0.7 convert_element_type.74
  2.1 0.7 convert_element_type.78
  2.8 1.2 %fusion.6 = f32[32]{0:T(128)S(1)} fusion(bf16[32,6144]{1,0:T(8,128)(2,1)} %hid_ref.1), kind=kLoop, calls=%fused_computation.11 | loop fusion | flops 589792 | bytes 393344 | tf_op jit(solution)/shard_map/reduce_sum | solution.py:33
  4.0 0.7 convert_element_type.70
  4.7 0.7 convert_element_type.68
  5.4 1.9 %fusion.5 = bf16[32,1,128]{2,0,1:T(8,128)(2,1)S(1)} fusion(bf16[6144,128]{1,0:T(8,128)(2,1)} %param.17, f32[128]{0:T(128)S(1)} %convert_element_type.74, bf16[32,6144]{1,0:T(8,128)(2,1)} %hid_ref.1, f32[6144]{0:T(1024)S(1)} %convert_element_type.68, f32[32]{0:T(128)S(1)} %add_rsqrt_fusion), kind=kOutput, calls=%fused_computation.8 | convolution fusion | flops 51126272 | bytes 1999488 | tf_op jit(solution)/shard_map/dot_general | solution.py:53
  7.3 0.1 slice_convert_fusion
  7.4 0.1 copy.49
  7.5 0.1 copy.60
  7.6 0.1 copy.59
  7.7 0.2 fusion.13
  7.9 0.1 copy.52
  7.9 0.1 copy.54
  8.1 0.1 fusion.18
  8.2 0.6 copy.56
  8.8 0.0 copy-done
  8.8 0.0 copy-done.2
  8.8 1.0 %fusion.21 = (f32[32,1,128]{2,0,1:T(8,128)S(1)}, bf16[32,1,128]{2,0,1:T(8,128)(2,1)}) fusion(f32[128]{0:T(128)S(1)} %convert_element_type.78, bf16[6144,128]{1,0:T(8,128)(2,1)S(1)} %copy-done, bf16[32,6144]{1,0:T(8,128)(2,1)S(1)} %copy-done.2, f32[6144]{0:T(1024)S(1)} %convert_element_type.68, f32[32]{0:T(128)S(1)} %add_rsqrt_fusion), kind=kOutput, calls=%fused_computation.36 | convolution fusion | flops 51130368 | bytes 2015872 | tf_op jit(solution)/shard_map/dot_general | solution.py:53
  9.8 0.1 multiply_cosine_fusion.1
  9.9 15.2 %fusion.1 = bf16[4,8,24,128]{3,1,2,0:T(8,128)(2,1)S(1)} fusion(bf16[6144,3072]{1,0:T(8,128)(2,1)} %param.15, f32[3072]{0:T(1024)S(1)} %convert_element_type.70, bf16[32,6144]{1,0:T(8,128)(2,1)S(1)} %copy-done.2, f32[6144]{0:T(1024)S(1)} %convert_element_type.68, f32[32]{0:T(128)S(1)} %add_rsqrt_fusion), kind=kOutput, calls=%fused_computation.2 | convolution fusion | flops 1208942592 | bytes 38375552 | tf_op jit(solution)/shard_map/dot_general | solution.py:53
  25.2 0.1 fusion.19
  25.3 0.3 copy.57
  25.6 0.1 convert.11
  25.7 0.1 subtract_convert_fusion
  25.8 0.1 pad_maximum_fusion.1
  25.9 0.3 copy.58
  26.2 0.0 copy-start.4
  26.2 0.2 pad_maximum_fusion
  26.3 0.5 copy.47
  26.8 0.1 copy.62
  26.9 0.1 pad.4.clone
  27.0 0.0 copy-done.4
  27.0 0.0 copy-start.3
  27.0 2.2 %copy-done.3 = bf16[32,512,1,128]{3,1,2,0:T(8,128)(2,1)S(1)} copy-done((bf16[32,512,1,128]{3,1,2,0:T(8,128)(2,1)S(1)}, bf16[32,512,1,128]{3,1,2,0:T(8,128)(2,1)}, u32[]{:S(2)}) %copy-start.3) | copy-done | bytes 4194328
  29.2 0.0 copy-start.1
  29.2 43.7 %tail.1 = bf16[32,6144]{1,0:T(8,128)(2,1)S(1)} custom-call(bf16[32,32,128]{2,1,0:T(8,128)(2,1)S(1)} %bitcast.21, f32[32,1,128]{2,1,0:T(1,128)S(1)} %get-tuple-element.18.kn_ref, f32[32,1,128]{2,1,0:T(1,128)S(1)} %bitcast.22, s32[32]{0:T(128)S(1)} %copy-done.4, bf16[32,6144]{1,0:T(8,128)(2,1)S(1)} %copy-done.2, bf16[32,512,128]{2,1,0:T(8,128)(2,1)S(1)} %bitcast.20, ...), custom_call_target="tpu_custom_call" | custom-call | tf_op jit(solution)/shard_map/tail/pallas_call | solution.py:273
  72.8 0.7 %copy.65 = bf16[32,6144]{1,0:T(8,128)(2,1)} copy(bf16[32,6144]{1,0:T(8,128)(2,1)S(1)} %tail.1) | data formatting | bytes 786432
  73.6 0.0 copy-done.1
  (6 shorter events, 0.1 us)
Async XLA Ops:
  0.6 8.1 %copy-start = (bf16[6144,128]{1,0:T(8,128)(2,1)S(1)}, bf16[6144,128]{1,0:T(8,128)(2,1)}, u32[]{:S(2)}) copy-start(bf16[6144,128]{1,0:T(8,128)(2,1)} %param.19) | copy-start | bytes 4718596
  0.6 8.1 %copy-start.2 = (bf16[32,6144]{1,0:T(8,128)(2,1)S(1)}, bf16[32,6144]{1,0:T(8,128)(2,1)}, u32[]{:S(2)}) copy-start(bf16[32,6144]{1,0:T(8,128)(2,1)} %hid_ref.1) | copy-start | bytes 1179652
  26.2 0.8 %copy-start.4 = (s32[32]{0:T(128)S(1)}, s32[32]{0:T(128)}, u32[]{:S(2)}) copy-start(s32[32]{0:T(128)} %seq_ref.1) | copy-start | bytes 388
  27.0 2.2 %copy-start.3 = (bf16[32,512,1,128]{3,1,2,0:T(8,128)(2,1)S(1)}, bf16[32,512,1,128]{3,1,2,0:T(8,128)(2,1)}, u32[]{:S(2)}) copy-start(bf16[32,512,1,128]{3,1,2,0:T(8,128)(2,1)} %param.22) | copy-start | bytes 12582916
  29.2 44.4 %copy-start.1 = (bf16[6144,128]{1,0:T(8,128)(2,1)S(1)}, bf16[6144,128]{1,0:T(8,128)(2,1)}, u32[]{:S(2)}) copy-start(bf16[6144,128]{1,0:T(8,128)(2,1)} %param.19) | copy-start | bytes 4718596

commit v2 on v1

--- a/solution.py
+++ b/solution.py
@@ -25,42 +25,24 @@
 N_OUT = 6144
 N_Z = 1536
 AG = 24
-UNROLL = 4
-
-
-def rms_norm(x_rows, norm_w):
-    x_f32 = x_rows.astype(jnp.float32)
-    mean_sq = jnp.mean(x_f32 * x_f32, axis=-1, keepdims=True)
-    return (x_f32 * lax.rsqrt(mean_sq + RMS_EPS) * norm_w.astype(jnp.float32)).astype(jnp.bfloat16)
-
-
-def apply_rotary(heads_in, positions):
-    rot_dim = heads_in.shape[-1] // 2
-    half_rot = rot_dim // 2
-    inv_freq = ROPE_BASE ** (-2.0 * jnp.arange(half_rot, dtype=jnp.float32) / rot_dim)
-    angles = positions.astype(jnp.float32)[:, None, None] * inv_freq
-    cos_t = jnp.cos(angles)
-    sin_t = jnp.sin(angles)
-    rot_pairs = heads_in[..., :rot_dim].astype(jnp.float32).reshape(heads_in.shape[:-1] + (half_rot, 2))
-    even_part = rot_pairs[..., 0]
-    odd_part = rot_pairs[..., 1]
-    rotated = jnp.stack([even_part * cos_t - odd_part * sin_t, even_part * sin_t + odd_part * cos_t], axis=-1)
-    rotated = rotated.reshape(heads_in.shape[:-1] + (rot_dim,)).astype(jnp.bfloat16)
-    return jnp.concatenate([rotated, heads_in[..., rot_dim:]], axis=-1)
-
-
-def project(normed, weight, bias_vec):
-    return (jnp.dot(normed, weight, preferred_element_type=jnp.float32) + bias_vec.astype(jnp.float32)).astype(jnp.bfloat16)
-
-
-def tail_kernel(q_ref, kn_ref, vn_ref, seq_ref, hid_ref, k_hbm, v_hbm, wo_hbm, y_ref,
+UNROLL = 8
+Q_DEV = 384
+K_CUT = 1536
+
+
+def step_kernel(hid_hbm, nw_ref, bq_ref, bk_ref, bv_ref, freq_ref, pos_ref, seq_ref,
+                wq_hbm, wk_hbm, wv_hbm, k_hbm, v_hbm, wo_hbm, y_ref, kn_ref, vn_ref,
+                hid_ref, normed, wqbuf, wkvbuf, q_all, kn_rows, vn_rows,
                 kbuf, vbuf, wobuf, o_send, o_recv, a_all, lhs, ypart, yrecv, ag,
+                hsem, wqsem, wkvsem, q_send, q_recv,
                 ksem, vsem, wsem, rs_send, rs_recv, z_send, z_recv, d_send, d_recv,
                 ag_send, ag_recv, f_send, f_recv):
     c = lax.axis_index('tp')
     s = lax.axis_index('sp')
     z = lax.div(s, PLANE)
     p = lax.rem(s, PLANE)
+    y_at = lax.div(p, 4)
+    x_at = lax.rem(p, 4)
     qk_scale = (D ** -0.5) * math.log2(math.e)
 
     def chip_of(i):
@@ -69,6 +51,16 @@
     def row_of(i):
         return chip_of(i) + PLANE * lax.rem(i, 2)
 
+    label = 4 * lax.rem(z, 2) + 2 * lax.rem(y_at, 2) + lax.rem(x_at, 2)
+    hid_copy = pltpu.make_async_copy(hid_hbm, hid_ref, hsem)
+    hid_copy.start()
+    q_cols = pl.ds(pl.multiple_of(label * Q_DEV, D), Q_DEV)
+    wq_copies = [pltpu.make_async_copy(
+        wq_hbm.at[pl.ds(K_CUT * j, K_CUT), q_cols], wqbuf.at[pl.ds(K_CUT * j, K_CUT)], wqsem.at[j])
+        for j in range(N_OUT // K_CUT)]
+    for cp in wq_copies:
+        cp.start()
+
     barrier = pltpu.get_barrier_semaphore()
 
     def greet(d, carry):
@@ -76,6 +68,11 @@
         return carry
     lax.fori_loop(1, SP, greet, 0)
     pl.semaphore_signal(barrier, inc=1, device_id={'tp': 1 - c}, device_id_type=MESH)
+
+    wkv_copies = [pltpu.make_async_copy(wk_hbm, wkvbuf.at[:, pl.ds(0, D)], wkvsem.at[0]),
+                  pltpu.make_async_copy(wv_hbm, wkvbuf.at[:, pl.ds(D, D)], wkvsem.at[1])]
+    for cp in wkv_copies:
+        cp.start()
 
     def k_copy(i):
         return pltpu.make_async_copy(k_hbm.at[row_of(i)], kbuf.at[i], ksem.at[i])
@@ -87,14 +84,74 @@
         k_copy(i).start()
         v_copy(i).start()
         return carry
-    lax.fori_loop(0, N_ROWS, start_kv, 0)
     wo_copies = [pltpu.make_async_copy(
         wo_hbm.at[pl.ds(768 * j, 768), pl.ds(pl.multiple_of(z * N_Z, N_Z), N_Z)],
         wobuf.at[pl.ds(768 * j, 768)], wsem.at[j]) for j in range(4)]
+
+    row_eye = lax.broadcasted_iota(jnp.int32, (N_ROWS, N_ROWS), 0) == lax.broadcasted_iota(jnp.int32, (N_ROWS, N_ROWS), 1)
+    pos_col = jnp.sum(jnp.where(row_eye, pos_ref[...].astype(F32), 0.0), axis=1, keepdims=True)
+    angles = pos_col * freq_ref[...]
+    is_even = lax.rem(lax.broadcasted_iota(jnp.int32, (N_ROWS, D), 1), 2) == 0
+    cos_t = jnp.cos(angles)
+    sin_t = jnp.where(is_even, -jnp.sin(angles), jnp.sin(angles))
+
+    def rotate(head):
+        other = jnp.where(is_even, pltpu.roll(head, D - 1, 1), pltpu.roll(head, 1, 1))
+        return (head * cos_t + other * sin_t).astype(BF16)
+
+    hid_copy.wait()
+    x_f32 = hid_ref[...].astype(F32)
+    mean_sq = jnp.mean(x_f32 * x_f32, axis=-1, keepdims=True)
+    normed[...] = (x_f32 * lax.rsqrt(mean_sq + RMS_EPS) * nw_ref[...].astype(F32)).astype(BF16)
+
+    q_mine = jnp.zeros((N_ROWS, Q_DEV), F32)
+    for j, cp in enumerate(wq_copies):
+        cp.wait()
+        cut = slice(K_CUT * j, K_CUT * (j + 1))
+        q_mine = q_mine + jnp.dot(normed[:, cut], wqbuf[cut, :], preferred_element_type=F32)
+    lax.fori_loop(0, N_ROWS, start_kv, 0)
     for cp in wo_copies:
         cp.start()
+    bias = jnp.zeros((1, Q_DEV), F32)
+    for j in range(8):
+        bias = jnp.where(label == j, bq_ref[:, j * Q_DEV:(j + 1) * Q_DEV].astype(F32), bias)
+    q_mine = (q_mine + bias).astype(BF16).astype(F32)
+    for hf in range(2):
+        q_all[pl.ds((hf * SLOT + HALF) * N_ROWS, (SLOT - HALF) * N_ROWS), :] = jnp.zeros(((SLOT - HALF) * N_ROWS, D), F32)
+
+    def q_rows(lab):
+        first = lax.div(lab, 4) * SLOT + 3 * lax.rem(lab, 4)
+        return pl.multiple_of(first * N_ROWS, N_ROWS)
+    for t in range(3):
+        q_all[pl.ds(q_rows(label) + t * N_ROWS, N_ROWS), :] = rotate(q_mine[:, t * D:(t + 1) * D]).astype(F32)
 
     pl.semaphore_wait(barrier, SP)
+
+    def across(v):
+        return lax.rem(v + 4 + (1 - 2 * lax.rem(v, 2)) * (1 - 2 * c), 4)
+    q_copies = []
+    for mask in range(7, 0, -1):
+        zd = across(z) if mask & 4 else z
+        yd = across(y_at) if mask & 2 else y_at
+        xd = across(x_at) if mask & 1 else x_at
+        mine = q_all.at[pl.ds(q_rows(label), 3 * N_ROWS)]
+        q_copies.append(pltpu.make_async_remote_copy(
+            src_ref=mine, dst_ref=mine, send_sem=q_send.at[mask - 1], recv_sem=q_recv.at[mask - 1],
+            device_id={'sp': zd * PLANE + yd * 4 + xd}, device_id_type=MESH))
+    for cp in q_copies:
+        cp.start()
+
+    for cp in wkv_copies:
+        cp.wait()
+    kv = jnp.dot(normed[...], wkvbuf[...], preferred_element_type=F32)
+    k_new = rotate((kv[:, :D] + bk_ref[...].astype(F32)).astype(BF16).astype(F32))
+    v_new = (kv[:, D:] + bv_ref[...].astype(F32)).astype(BF16)
+    kn_ref[...] = k_new
+    vn_ref[...] = v_new
+    kn_rows[...] = k_new.astype(F32)
+    vn_rows[...] = v_new.astype(F32)
+    for cp in q_copies:
+        cp.wait_recv()
 
     lane = lax.broadcasted_iota(jnp.int32, (SLOT, D), 1)
     sub = lax.broadcasted_iota(jnp.int32, (SLOT, D), 0)
@@ -114,7 +171,7 @@
         scores = []
         for i, b in zip(idx, rows):
             k_copy(i).wait()
-            sc = lax.dot_general(q_ref[b], kbuf[i], (((1,), (1,)), ((), ())), preferred_element_type=F32)
+            sc = lax.dot_general(q_all[pl.ds(b, 2 * SLOT, stride=N_ROWS), :].astype(BF16), kbuf[i], (((1,), (1,)), ((), ())), preferred_element_type=F32)
             scores.append(jnp.where(pos < seq_ref[b], sc, NEG_BIG))
         tops = [jnp.max(sc, axis=1, keepdims=True) for sc in scores]
         probs = [jnp.exp2((sc - m) * qk_scale) for sc, m in zip(scores, tops)]
@@ -144,10 +201,10 @@
 
     my_row = p + PLANE * lax.div(z, 2)
     my_half = lax.rem(z, 2)
-    q_mine = q_ref[my_row, pl.ds(pl.multiple_of(my_half * SLOT, SLOT), SLOT), :].astype(F32)
-    k_mine = kn_ref[my_row]
-    v_mine = vn_ref[my_row]
-    s_new = jnp.sum(q_mine * k_mine, axis=1, keepdims=True) * qk_scale
+    q_own = q_all[pl.ds(my_half * SLOT * N_ROWS + my_row, SLOT, stride=N_ROWS), :]
+    k_mine = kn_rows[pl.ds(my_row, 1), :]
+    v_mine = vn_rows[pl.ds(my_row, 1), :]
+    s_new = jnp.sum(q_own * k_mine, axis=1, keepdims=True) * qk_scale
 
     def all_in(ref, sem):
         pltpu.make_async_copy(ref, ref, sem).wait()
@@ -248,7 +305,7 @@
                 y_ref[rows, col] = (hid_ref[rows, col].astype(F32) + y_blk).astype(BF16)
 
     all_in(o_send.at[pl.ds(0, SP - 1)], rs_send)
-    for cp in z_copies:
+    for cp in q_copies + z_copies:
         cp.wait_send()
     d_copy.wait_send()
 
@@ -266,16 +323,26 @@
     lax.fori_loop(0, SP // 2, drain, 0)
 
 
-def tail(q_pad, k_new, v_new, seq_lens, hidden, k_cache, v_cache, w_o):
+def step_call(freq, *operands):
+    hidden, norm_w, w_q, b_q, w_k, b_k, w_v, b_v, w_o, k_cache, v_cache, positions, seq_lens = operands
     vmem = pl.BlockSpec(memory_space=pltpu.VMEM)
+    smem = pl.BlockSpec(memory_space=pltpu.SMEM)
     hbm = pl.BlockSpec(memory_space=pl.ANY)
     dma = pltpu.SemaphoreType.DMA
     return pl.pallas_call(
-        tail_kernel,
-        out_shape=jax.ShapeDtypeStruct((N_ROWS, N_OUT), BF16),
-        in_specs=[vmem, vmem, vmem, pl.BlockSpec(memory_space=pltpu.SMEM), vmem, hbm, hbm, hbm],
-        out_specs=vmem,
+        step_kernel,
+        out_shape=(jax.ShapeDtypeStruct((N_ROWS, N_OUT), BF16),
+                   jax.ShapeDtypeStruct((N_ROWS, D), BF16), jax.ShapeDtypeStruct((N_ROWS, D), BF16)),
+        in_specs=[hbm, vmem, vmem, vmem, vmem, vmem, vmem, smem, hbm, hbm, hbm, hbm, hbm, hbm],
+        out_specs=(vmem, vmem, vmem),
         scratch_shapes=[
+            pltpu.VMEM((N_ROWS, N_OUT), BF16),
+            pltpu.VMEM((N_ROWS, N_OUT), BF16),
+            pltpu.VMEM((N_OUT, Q_DEV), BF16),
+            pltpu.VMEM((N_OUT, 2 * D), BF16),
+            pltpu.VMEM((2 * SLOT * N_ROWS, D), F32),
+            pltpu.VMEM((N_ROWS, D), F32),
+            pltpu.VMEM((N_ROWS, D), F32),
             pltpu.VMEM((N_ROWS, S_DEV, D), BF16),
             pltpu.VMEM((N_ROWS, S_DEV, D), BF16),
             pltpu.VMEM((3072, N_Z), BF16),
@@ -286,28 +353,25 @@
             pltpu.VMEM((2, 8, N_Z), F32),
             pltpu.VMEM((AG, D), F32),
             pltpu.VMEM((SP * AG, D), F32),
+            dma, dma((N_OUT // K_CUT,)), dma((2,)), dma((7,)), dma((7,)),
             dma((N_ROWS,)), dma((N_ROWS,)), dma((4,)),
             dma, dma, dma((3,)), dma((3,)), dma, dma,
             dma((SP // 2,)), dma((SP // 2,)), dma((SP // 2,)), dma((SP // 2,)),
         ],
         compiler_params=pltpu.CompilerParams(
-            collective_id=0, has_side_effects=True, vmem_limit_bytes=48 * 1024 * 1024),
-        name='tail',
-    )(q_pad, k_new, v_new, seq_lens, hidden, k_cache, v_cache, w_o)
+            collective_id=0, has_side_effects=True, vmem_limit_bytes=56 * 1024 * 1024),
+        name='decode_step',
+    )(hidden, norm_w.reshape(1, -1), b_q.reshape(1, -1), b_k.reshape(1, -1), b_v.reshape(1, -1), freq,
+      positions.reshape(1, -1), seq_lens, w_q, w_k, w_v,
+      k_cache.reshape(N_ROWS, S_DEV, D), v_cache.reshape(N_ROWS, S_DEV, D), w_o)
 
 
 def solution(mesh):
-    def device_step(hidden, norm_w, w_q, b_q, w_k, b_k, w_v, b_v, w_o, k_cache, v_cache, positions, seq_lens):
-        n_rows = hidden.shape[0]
-        normed = rms_norm(hidden, norm_w)
-        q_rot = apply_rotary(project(normed, w_q, b_q).reshape(n_rows, 24, D), positions)
-        k_rot = apply_rotary(project(normed, w_k, b_k).reshape(n_rows, 1, D), positions)
-        v_new = project(normed, w_v, b_v).reshape(n_rows, 1, D)
-        q_pad = jnp.pad(q_rot.reshape(n_rows, 2, HALF, D), ((0, 0), (0, 0), (0, SLOT - HALF), (0, 0)))
-        q_pad = q_pad.reshape(n_rows, 2 * SLOT, D)
-        y_out = tail(q_pad, k_rot.astype(F32), v_new.astype(F32), seq_lens, hidden,
-                     k_cache.reshape(n_rows, S_DEV, D), v_cache.reshape(n_rows, S_DEV, D), w_o)
-        return y_out, k_rot, v_new
+    def device_step(*operands):
+        inv_freq = ROPE_BASE ** (-2.0 * jnp.arange(D // 4, dtype=jnp.float32) / (D // 2))
+        freq = jnp.pad(jnp.repeat(inv_freq, 2), (0, D // 2)).reshape(1, D)
+        y_out, k_new, v_new = step_call(freq, *operands)
+        return y_out, k_new.reshape(N_ROWS, 1, D), v_new.reshape(N_ROWS, 1, D)
 
     col_spec = P(None, 'tp')
     vec_spec = P('tp')

time: 73.9 us -> 57.5 us (0.78)
  matrix products: 18.2 us -> 0 us
  other arithmetic: 5.62 us -> 0.01 us
  Pallas kernels: 43.7 us -> 48.6 us
  local copies, waits for them, and re-layouts: 5.32 us -> 7.68 us
    dot_general x3 -> x0, matrix products: 18.2 us -> none  [project(): jnp.dot(normed, weight, preferred_element_type=jnp.float32)]
    pallas_call x1, Pallas kernels: 43.7 us -> 48.6 us  [step_call(): pl.pallas_call(step_kernel, out_shape=(jax.ShapeDtypeStruct((N_ROWS, N_OU...]
    convert_element_type x7 -> x0, other arithmetic: 3.65 us -> none  [the longest x3 2.02 us: project(): bias_vec.astype(jnp.float32)]
    reshape x1 -> x4, local copies, waits for them, and re-layouts: 0.08 us -> 3.25 us  [the longest x1 1.33 us: step_call(): norm_w.reshape(1, -1)]
    reduce_sum x1 -> x0, other arithmetic: 1.18 us -> none  [rms_norm(): mean_sq = jnp.mean(x_f32 * x_f32, axis=-1, keepdims=True)]
    unnamed x19 -> x3, local copies, waits for them, and re-layouts: 4.39 us -> 4.36 us
where the time goes in v2:
time: 57.5 us; the launch traced here: 57 us
  Pallas kernels  48.6 us (85%)
  local copies, waits for them, and re-layouts  7.68 us (13%)
  between operations  0.65 us (1%)
    pallas_call x1, Pallas kernels, step_call(): pl.pallas_call(step_kernel, out_shape=(jax.ShapeDtypeStruct((N_ROWS, N_OU...  48.6 us
    unnamed x3, local copies, waits for them, and re-layouts  4.36 us
    reshape x1, local copies, waits for them, and re-layouts, step_call(): norm_w.reshape(1, -1)  1.33 us
    reshape x1, local copies, waits for them, and re-layouts, step_call(): b_q.reshape(1, -1)  1.3 us

profile of v2, /device:TPU:1, one launch (start us, length us, event | category | flops | bytes accessed | tf_op | source)
XLA Modules:
  0.0 57.0 jit_solution(145645937897937484)
XLA Ops:
  0.6 1.3 %reshape.40.bq_ref = bf16[1,3072]{1,0:T(2,128)(2,1)} reshape(bf16[3072]{0:T(1024)(128)(2,1)} %param.16) | data formatting | bytes 12288 | tf_op jit(solution)/shard_map/reshape | solution.py:364
  1.9 0.1 broadcast_in_dim.3
  2.0 0.1 reshape.43
  2.1 0.5 pad_bitcast_fusion.freq_ref
  2.6 1.3 %reshape.39.nw_ref = bf16[1,6144]{1,0:T(2,128)(2,1)} reshape(bf16[6144]{0:T(1024)(128)(2,1)} %param.14) | data formatting | bytes 24576 | tf_op jit(solution)/shard_map/reshape | solution.py:364
  4.0 48.6 %decode_step.1 = (bf16[32,6144]{1,0:T(8,128)(2,1)}, bf16[32,128]{1,0:T(8,128)(2,1)}, bf16[32,128]{1,0:T(8,128)(2,1)}) custom-call(bf16[32,6144]{1,0:T(8,128)(2,1)} %hid_hbm.1, bf16[1,6144]{1,0:T(2,128)(2,1)} %reshape.39.nw_ref, bf16[1,3072]{1,0:T(2,128)(2,1)} %reshape.40.bq_ref, bf16[1,128]{1,0:T(2,128)(2,1)} %bitcast.13, bf16[1,128]{1,0:T(2,128)(2,1)} %bitcast.14, ...), custom_call_target="tpu_custom_call" | custom-call | tf_op jit(solution)/shard_map/decode_step/pallas_call | solution.py:332
  52.6 1.8 %copy.19 = bf16[32,6144]{1,0:T(8,128)(2,1)} copy(bf16[32,6144]{1,0:T(8,128)(2,1)} %get-tuple-element.12) | data formatting | bytes 786432
  54.4 1.3 %copy.20 = bf16[32,1,128]{2,0,1:T(8,128)(2,1)} copy(bf16[32,1,128]{2,0,1:T(8,128)(2,1)} %bitcast.12) | data formatting | bytes 16384
  55.7 1.3 %copy.21 = bf16[32,1,128]{2,0,1:T(8,128)(2,1)} copy(bf16[32,1,128]{2,0,1:T(8,128)(2,1)} %bitcast.11) | data formatting | bytes 16384
  (1 shorter events, 0.0 us)

commit v3 on v2

--- a/solution.py
+++ b/solution.py
@@ -25,16 +25,15 @@
 N_OUT = 6144
 N_Z = 1536
 AG = 24
-UNROLL = 8
 Q_DEV = 384
 K_CUT = 1536
 
 
-def step_kernel(hid_hbm, nw_ref, bq_ref, bk_ref, bv_ref, freq_ref, pos_ref, seq_ref,
-                wq_hbm, wk_hbm, wv_hbm, k_hbm, v_hbm, wo_hbm, y_ref, kn_ref, vn_ref,
-                hid_ref, normed, wqbuf, wkvbuf, q_all, kn_rows, vn_rows,
-                kbuf, vbuf, wobuf, o_send, o_recv, a_all, lhs, ypart, yrecv, ag,
-                hsem, wqsem, wkvsem, q_send, q_recv,
+def step_kernel(hid_hbm, nw_hbm, bq_hbm, bk_hbm, bv_hbm, freq_ref, pos_hbm, seq_hbm,
+                wq_hbm, wk_hbm, wv_hbm, k_hbm, v_hbm, wo_hbm, ag, kn_rows, vn_rows,
+                nw_ref, bq_ref, bk_ref, bv_ref, pos_ref, seq_ref, hid_ref, normed, wqbuf, wkvbuf, bq_rows, q_all,
+                kbuf, vbuf, wobuf, o_send, o_recv, a_all, lhs, ypart, yrecv,
+                vecsem, hsem, wqsem, wkvsem, q_send, q_recv,
                 ksem, vsem, wsem, rs_send, rs_recv, z_send, z_recv, d_send, d_recv,
                 ag_send, ag_recv, f_send, f_recv):
     c = lax.axis_index('tp')
@@ -45,15 +44,13 @@
     x_at = lax.rem(p, 4)
     qk_scale = (D ** -0.5) * math.log2(math.e)
 
-    def chip_of(i):
-        return lax.rem(p + 1 + lax.div(i, 2), PLANE)
-
-    def row_of(i):
-        return chip_of(i) + PLANE * lax.rem(i, 2)
-
     label = 4 * lax.rem(z, 2) + 2 * lax.rem(y_at, 2) + lax.rem(x_at, 2)
     hid_copy = pltpu.make_async_copy(hid_hbm, hid_ref, hsem)
     hid_copy.start()
+    vec_copies = [pltpu.make_async_copy(src, dst, vecsem.at[j]) for j, (src, dst) in enumerate((
+        (pos_hbm, pos_ref), (nw_hbm, nw_ref), (bq_hbm, bq_ref), (bk_hbm, bk_ref), (bv_hbm, bv_ref), (seq_hbm, seq_ref)))]
+    for cp in vec_copies:
+        cp.start()
     q_cols = pl.ds(pl.multiple_of(label * Q_DEV, D), Q_DEV)
     wq_copies = [pltpu.make_async_copy(
         wq_hbm.at[pl.ds(K_CUT * j, K_CUT), q_cols], wqbuf.at[pl.ds(K_CUT * j, K_CUT)], wqsem.at[j])
@@ -74,20 +71,19 @@
     for cp in wkv_copies:
         cp.start()
 
-    def k_copy(i):
-        return pltpu.make_async_copy(k_hbm.at[row_of(i)], kbuf.at[i], ksem.at[i])
-
-    def v_copy(i):
-        return pltpu.make_async_copy(v_hbm.at[row_of(i)], vbuf.at[i], vsem.at[i])
-
-    def start_kv(i, carry):
-        k_copy(i).start()
-        v_copy(i).start()
-        return carry
+    def kv_copies(step):
+        y_to = lax.rem(y_at + 1 + step, 4)
+        pairs = []
+        for r in range(2):
+            rows = pl.ds(PLANE * r + 4 * y_to, 4)
+            pairs.append(pltpu.make_async_copy(k_hbm.at[rows], kbuf.at[rows], ksem.at[2 * step + r]))
+            pairs.append(pltpu.make_async_copy(v_hbm.at[rows], vbuf.at[rows], vsem.at[2 * step + r]))
+        return pairs
     wo_copies = [pltpu.make_async_copy(
         wo_hbm.at[pl.ds(768 * j, 768), pl.ds(pl.multiple_of(z * N_Z, N_Z), N_Z)],
         wobuf.at[pl.ds(768 * j, 768)], wsem.at[j]) for j in range(4)]
 
+    vec_copies[0].wait()
     row_eye = lax.broadcasted_iota(jnp.int32, (N_ROWS, N_ROWS), 0) == lax.broadcasted_iota(jnp.int32, (N_ROWS, N_ROWS), 1)
     pos_col = jnp.sum(jnp.where(row_eye, pos_ref[...].astype(F32), 0.0), axis=1, keepdims=True)
     angles = pos_col * freq_ref[...]
@@ -100,22 +96,27 @@
         return (head * cos_t + other * sin_t).astype(BF16)
 
     hid_copy.wait()
+    for cp in vec_copies[1:]:
+        cp.wait()
     x_f32 = hid_ref[...].astype(F32)
     mean_sq = jnp.mean(x_f32 * x_f32, axis=-1, keepdims=True)
-    normed[...] = (x_f32 * lax.rsqrt(mean_sq + RMS_EPS) * nw_ref[...].astype(F32)).astype(BF16)
+    unit = lax.rsqrt(mean_sq + RMS_EPS)
+    nw_rows = nw_ref[...].astype(F32)
+    for j in range(N_OUT // D):
+        cut = slice(j * D, (j + 1) * D)
+        normed[:, cut] = (x_f32[:, cut] * unit * nw_rows[j:j + 1, :]).astype(BF16)
+    bq_rows[...] = bq_ref[...].astype(F32)
 
     q_mine = jnp.zeros((N_ROWS, Q_DEV), F32)
     for j, cp in enumerate(wq_copies):
         cp.wait()
         cut = slice(K_CUT * j, K_CUT * (j + 1))
         q_mine = q_mine + jnp.dot(normed[:, cut], wqbuf[cut, :], preferred_element_type=F32)
-    lax.fori_loop(0, N_ROWS, start_kv, 0)
+    for step in range(4):
+        for cp in kv_copies(step):
+            cp.start()
     for cp in wo_copies:
         cp.start()
-    bias = jnp.zeros((1, Q_DEV), F32)
-    for j in range(8):
-        bias = jnp.where(label == j, bq_ref[:, j * Q_DEV:(j + 1) * Q_DEV].astype(F32), bias)
-    q_mine = (q_mine + bias).astype(BF16).astype(F32)
     for hf in range(2):
         q_all[pl.ds((hf * SLOT + HALF) * N_ROWS, (SLOT - HALF) * N_ROWS), :] = jnp.zeros(((SLOT - HALF) * N_ROWS, D), F32)
 
@@ -123,7 +124,8 @@
         first = lax.div(lab, 4) * SLOT + 3 * lax.rem(lab, 4)
         return pl.multiple_of(first * N_ROWS, N_ROWS)
     for t in range(3):
-        q_all[pl.ds(q_rows(label) + t * N_ROWS, N_ROWS), :] = rotate(q_mine[:, t * D:(t + 1) * D]).astype(F32)
+        head = q_mine[:, t * D:(t + 1) * D] + bq_rows[pl.ds(3 * label + t, 1), :]
+        q_all[pl.ds(q_rows(label) + t * N_ROWS, N_ROWS), :] = rotate(head.astype(BF16).astype(F32)).astype(F32)
 
     pl.semaphore_wait(barrier, SP)
 
@@ -146,8 +148,6 @@
     kv = jnp.dot(normed[...], wkvbuf[...], preferred_element_type=F32)
     k_new = rotate((kv[:, :D] + bk_ref[...].astype(F32)).astype(BF16).astype(F32))
     v_new = (kv[:, D:] + bv_ref[...].astype(F32)).astype(BF16)
-    kn_ref[...] = k_new
-    vn_ref[...] = v_new
     kn_rows[...] = k_new.astype(F32)
     vn_rows[...] = v_new.astype(F32)
     for cp in q_copies:
@@ -158,46 +158,50 @@
     eye = lane == sub
     pos = s * S_DEV + lax.broadcasted_iota(jnp.int32, (2 * SLOT, S_DEV), 1)
 
-    def rs_copy(i, hf):
-        dest = (2 * lax.rem(i, 2) + hf) * PLANE + chip_of(i)
-        slot = 2 * i + hf
-        return dest, pltpu.make_async_remote_copy(
-            src_ref=o_send.at[slot], dst_ref=o_recv.at[pl.ds(pl.multiple_of(s * SLOT, SLOT), SLOT)],
+    def rs_copy(dest):
+        return pltpu.make_async_remote_copy(
+            src_ref=o_send.at[dest], dst_ref=o_recv.at[pl.ds(pl.multiple_of(s * SLOT, SLOT), SLOT)],
             send_sem=rs_send, recv_sem=rs_recv, device_id={'sp': dest}, device_id_type=MESH)
 
-    def rows_step(g, carry):
-        idx = [g * UNROLL + u for u in range(UNROLL)]
-        rows = [row_of(i) for i in idx]
+    def rows_step(step, carry):
+        y_to = lax.rem(y_at + 1 + step, 4)
+        for cp in kv_copies(step):
+            cp.wait()
+        work = []
+        for u in range(4):
+            for r in range(2):
+                chip = 4 * y_to + lax.rem(x_at + 1 + u, 4)
+                work.append((u, r, chip, chip + PLANE * r))
         scores = []
-        for i, b in zip(idx, rows):
-            k_copy(i).wait()
-            sc = lax.dot_general(q_all[pl.ds(b, 2 * SLOT, stride=N_ROWS), :].astype(BF16), kbuf[i], (((1,), (1,)), ((), ())), preferred_element_type=F32)
+        for u, r, chip, b in work:
+            sc = lax.dot_general(q_all[pl.ds(b, 2 * SLOT, stride=N_ROWS), :].astype(BF16), kbuf[b],
+                                 (((1,), (1,)), ((), ())), preferred_element_type=F32)
             scores.append(jnp.where(pos < seq_ref[b], sc, NEG_BIG))
         tops = [jnp.max(sc, axis=1, keepdims=True) for sc in scores]
         probs = [jnp.exp2((sc - m) * qk_scale) for sc, m in zip(scores, tops)]
         sums = [jnp.sum(pr, axis=1, keepdims=True) for pr in probs]
-        for i, m, l, pr in zip(idx, tops, sums, probs):
-            v_copy(i).wait()
-            o = jnp.dot(pr.astype(BF16), vbuf[i], preferred_element_type=F32)
+        for (u, r, chip, b), m, l, pr in zip(work, tops, sums, probs):
+            o = jnp.dot(pr.astype(BF16), vbuf[b], preferred_element_type=F32)
             m2 = m * qk_scale
             for hf in range(2):
                 part = slice(hf * SLOT, (hf + 1) * SLOT)
                 m_row = jnp.sum(jnp.where(eye, m2[part], 0.0), axis=0, keepdims=True)
                 l_row = jnp.sum(jnp.where(eye, l[part], 0.0), axis=0, keepdims=True)
-                o_send[2 * i + hf] = jnp.where(sub == HALF, m_row, jnp.where(sub == HALF + 1, l_row, o[part]))
-        for i in idx:
+                o_send[(2 * r + hf) * PLANE + chip] = jnp.where(
+                    sub == HALF, m_row, jnp.where(sub == HALF + 1, l_row, o[part]))
+        for u, r, chip, b in work:
             for hf in range(2):
-                dest, cp = rs_copy(i, hf)
-
-                @pl.when(dest != s)
-                def _():
-                    cp.start()
-
-                @pl.when(dest == s)
-                def _():
-                    o_recv[pl.ds(pl.multiple_of(s * SLOT, SLOT), SLOT), :] = o_send[2 * i + hf]
-        return carry
-    lax.fori_loop(0, N_ROWS // UNROLL, rows_step, 0)
+                dest = (2 * r + hf) * PLANE + chip
+                if u < 3:
+                    rs_copy(dest).start()
+                else:
+                    @pl.when(dest != s)
+                    def _():
+                        rs_copy(dest).start()
+        return carry
+    lax.fori_loop(0, 4, rows_step, 0)
+    mine = pl.ds(pl.multiple_of(s * SLOT, SLOT), SLOT)
+    o_recv[mine, :] = o_send[s]
 
     my_row = p + PLANE * lax.div(z, 2)
     my_half = lax.rem(z, 2)
@@ -296,14 +300,6 @@
         return carry
     lax.fori_loop(0, SP // 2, relayed, 0)
 
-    for zz in range(4):
-        for blk in range(12):
-            col = slice(zz * N_Z + blk * D, zz * N_Z + (blk + 1) * D)
-            for r in range(2):
-                rows = slice(PLANE * r, PLANE * (r + 1))
-                y_blk = ag[pl.ds(zz * PLANE * AG + r * 12 + blk, PLANE, stride=AG), :]
-                y_ref[rows, col] = (hid_ref[rows, col].astype(F32) + y_blk).astype(BF16)
-
     all_in(o_send.at[pl.ds(0, SP - 1)], rs_send)
     for cp in q_copies + z_copies:
         cp.wait_send()
@@ -326,23 +322,27 @@
 def step_call(freq, *operands):
     hidden, norm_w, w_q, b_q, w_k, b_k, w_v, b_v, w_o, k_cache, v_cache, positions, seq_lens = operands
     vmem = pl.BlockSpec(memory_space=pltpu.VMEM)
-    smem = pl.BlockSpec(memory_space=pltpu.SMEM)
-    hbm = pl.BlockSpec(memory_space=pl.ANY)
+    hbm = pl.BlockSpec(memory_space=pltpu.HBM)
     dma = pltpu.SemaphoreType.DMA
     return pl.pallas_call(
         step_kernel,
-        out_shape=(jax.ShapeDtypeStruct((N_ROWS, N_OUT), BF16),
-                   jax.ShapeDtypeStruct((N_ROWS, D), BF16), jax.ShapeDtypeStruct((N_ROWS, D), BF16)),
-        in_specs=[hbm, vmem, vmem, vmem, vmem, vmem, vmem, smem, hbm, hbm, hbm, hbm, hbm, hbm],
+        out_shape=(jax.ShapeDtypeStruct((SP * AG, D), F32),
+                   jax.ShapeDtypeStruct((N_ROWS, D), F32), jax.ShapeDtypeStruct((N_ROWS, D), F32)),
+        in_specs=[hbm, hbm, hbm, hbm, hbm, vmem, hbm, hbm, hbm, hbm, hbm, hbm, hbm, hbm],
         out_specs=(vmem, vmem, vmem),
         scratch_shapes=[
+            pltpu.VMEM((N_OUT // D, D), BF16),
+            pltpu.VMEM((24, D), BF16),
+            pltpu.VMEM((1, D), BF16),
+            pltpu.VMEM((1, D), BF16),
+            pltpu.VMEM((1, N_ROWS), jnp.int32),
+            pltpu.SMEM((N_ROWS,), jnp.int32),
             pltpu.VMEM((N_ROWS, N_OUT), BF16),
             pltpu.VMEM((N_ROWS, N_OUT), BF16),
             pltpu.VMEM((N_OUT, Q_DEV), BF16),
             pltpu.VMEM((N_OUT, 2 * D), BF16),
+            pltpu.VMEM((24, D), F32),
             pltpu.VMEM((2 * SLOT * N_ROWS, D), F32),
-            pltpu.VMEM((N_ROWS, D), F32),
-            pltpu.VMEM((N_ROWS, D), F32),
             pltpu.VMEM((N_ROWS, S_DEV, D), BF16),
             pltpu.VMEM((N_ROWS, S_DEV, D), BF16),
             pltpu.VMEM((3072, N_Z), BF16),
@@ -352,25 +352,50 @@
             pltpu.VMEM((8, 3072), F32),
             pltpu.VMEM((2, 8, N_Z), F32),
             pltpu.VMEM((AG, D), F32),
-            pltpu.VMEM((SP * AG, D), F32),
-            dma, dma((N_OUT // K_CUT,)), dma((2,)), dma((7,)), dma((7,)),
-            dma((N_ROWS,)), dma((N_ROWS,)), dma((4,)),
+            dma((6,)), dma, dma((N_OUT // K_CUT,)), dma((2,)), dma((7,)), dma((7,)),
+            dma((8,)), dma((8,)), dma((4,)),
             dma, dma, dma((3,)), dma((3,)), dma, dma,
             dma((SP // 2,)), dma((SP // 2,)), dma((SP // 2,)), dma((SP // 2,)),
         ],
         compiler_params=pltpu.CompilerParams(
-            collective_id=0, has_side_effects=True, vmem_limit_bytes=56 * 1024 * 1024),
+            collective_id=0, has_side_effects=True, vmem_limit_bytes=36 * 1024 * 1024),
         name='decode_step',
-    )(hidden, norm_w.reshape(1, -1), b_q.reshape(1, -1), b_k.reshape(1, -1), b_v.reshape(1, -1), freq,
-      positions.reshape(1, -1), seq_lens, w_q, w_k, w_v,
-      k_cache.reshape(N_ROWS, S_DEV, D), v_cache.reshape(N_ROWS, S_DEV, D), w_o)
+    )(*(x if x is freq else pltpu.with_memory_space_constraint(x, pltpu.HBM) for x in (
+        hidden, norm_w.reshape(-1, D), b_q.reshape(-1, D), b_k.reshape(1, -1), b_v.reshape(1, -1), freq,
+        positions.reshape(1, -1), seq_lens, w_q, w_k, w_v,
+        k_cache.reshape(N_ROWS, S_DEV, D), v_cache.reshape(N_ROWS, S_DEV, D), w_o)))
+
+
+def finish_kernel(ag, kn_rows, vn_rows, hid_ref, y_ref, kn_ref, vn_ref):
+    kn_ref[...] = kn_rows[...].astype(BF16)
+    vn_ref[...] = vn_rows[...].astype(BF16)
+    for zz in range(4):
+        for blk in range(12):
+            col = slice(zz * N_Z + blk * D, zz * N_Z + (blk + 1) * D)
+            for r in range(2):
+                rows = slice(PLANE * r, PLANE * (r + 1))
+                y_blk = ag[pl.ds(zz * PLANE * AG + r * 12 + blk, PLANE, stride=AG), :]
+                y_ref[rows, col] = (hid_ref[rows, col].astype(F32) + y_blk).astype(BF16)
+
+
+def finish(ag, kn_rows, vn_rows, hidden):
+    vmem = pl.BlockSpec(memory_space=pltpu.VMEM)
+    return pl.pallas_call(
+        finish_kernel,
+        out_shape=(jax.ShapeDtypeStruct((N_ROWS, N_OUT), BF16),
+                   jax.ShapeDtypeStruct((N_ROWS, D), BF16), jax.ShapeDtypeStruct((N_ROWS, D), BF16)),
+        in_specs=[vmem] * 4, out_specs=(vmem,) * 3,
+        compiler_params=pltpu.CompilerParams(vmem_limit_bytes=8 * 1024 * 1024),
+        name='finish',
+    )(ag, kn_rows, vn_rows, hidden)
 
 
 def solution(mesh):
     def device_step(*operands):
-        inv_freq = ROPE_BASE ** (-2.0 * jnp.arange(D // 4, dtype=jnp.float32) / (D // 2))
-        freq = jnp.pad(jnp.repeat(inv_freq, 2), (0, D // 2)).reshape(1, D)
-        y_out, k_new, v_new = step_call(freq, *operands)
+        lane = jnp.arange(D, dtype=jnp.int32)
+        inv_freq = ROPE_BASE ** (-2.0 * (lane // 2).astype(jnp.float32) / (D // 2))
+        freq = jnp.where(lane < D // 2, inv_freq, 0.0).reshape(1, D)
+        y_out, k_new, v_new = finish(*step_call(freq, *operands), operands[0])
         return y_out, k_new.reshape(N_ROWS, 1, D), v_new.reshape(N_ROWS, 1, D)
 
     col_spec = P(None, 'tp')

time: 57.5 us -> 43.1 us (0.75)
  local copies, waits for them, and re-layouts: 7.68 us -> 0.01 us
  Pallas kernels: 48.6 us -> 42.2 us
    pallas_call x1 -> x2, Pallas kernels: 48.6 us -> 42.2 us  [the longest x1 41.3 us: step_call(): pl.pallas_call(step_kernel, out_shape=(jax.ShapeDtypeStruct((SP * AG, D),...]
    unnamed x3 -> x2, local copies, waits for them, and re-layouts: 4.36 us -> 0.01 us
    reshape x4 -> x0, local copies, waits for them, and re-layouts: 3.25 us -> none  [the longest x1 1.33 us: step_call(): norm_w.reshape(1, -1)]
where the time goes in v3:
time: 43.1 us; the launch traced here: 42.9 us
  Pallas kernels  42.2 us (98%)
  between operations  0.66 us (2%)
    pallas_call x1, Pallas kernels, step_call(): pl.pallas_call(step_kernel, out_shape=(jax.ShapeDtypeStruct((SP * AG, D),...  41.3 us
    pallas_call x1, Pallas kernels, finish(): pl.pallas_call(finish_kernel, out_shape=(jax.ShapeDtypeStruct((N_ROWS, N_...  0.92 us

profile of v3, /device:TPU:1, one launch (start us, length us, event | category | flops | bytes accessed | tf_op | source)
XLA Modules:
  0.0 42.9 jit_solution(13264013608098812928)
XLA Ops:
  0.6 0.0 copy-start
  0.7 41.3 %decode_step.1 = (f32[1536,128]{1,0:T(8,128)S(1)}, f32[32,128]{1,0:T(8,128)S(1)}, f32[32,128]{1,0:T(8,128)S(1)}) custom-call(bf16[32,6144]{1,0:T(8,128)(2,1)} %hid_ref.1, bf16[48,128]{1,0:T(8,128)(2,1)} %bitcast.11, bf16[24,128]{1,0:T(8,128)(2,1)} %bitcast.12, bf16[1,128]{1,0:T(2,128)(2,1)} %bitcast.13, bf16[1,128]{1,0:T(2,128)(2,1)} %bitcast.14, ...), custom_call_target="tpu_custom_call" | custom-call | tf_op jit(solution)/shard_map/decode_step/pallas_call | solution.py:327
  42.0 0.0 copy-done
  42.0 0.9 %finish.1 = (bf16[32,6144]{1,0:T(8,128)(2,1)}, bf16[32,128]{1,0:T(8,128)(2,1)}, bf16[32,128]{1,0:T(8,128)(2,1)}) custom-call(f32[1536,128]{1,0:T(8,128)S(1)} %get-tuple-element.9.ag, f32[32,128]{1,0:T(8,128)S(1)} %get-tuple-element.10.kn_rows, f32[32,128]{1,0:T(8,128)S(1)} %get-tuple-element.11.vn_rows, bf16[32,6144]{1,0:T(8,128)(2,1)S(1)} %copy-done), custom_call_target="tpu_custom_call" | custom-call | tf_op jit(solution)/shard_map/finish/pallas_call | solution.py:383
  (1 shorter events, 0.0 us)
Async XLA Ops:
  0.6 41.3 %copy-start = (bf16[32,6144]{1,0:T(8,128)(2,1)S(1)}, bf16[32,6144]{1,0:T(8,128)(2,1)}, u32[]{:S(2)}) copy-start(bf16[32,6144]{1,0:T(8,128)(2,1)} %hid_ref.1) | copy-start | bytes 1179652

commit v4 on v3

v4 whole, which is shorter than its diff:
```python
import functools
import math

import jax
import jax.numpy as jnp
from jax import lax
from jax.experimental import pallas as pl
from jax.experimental.pallas import tpu as pltpu
from jax.sharding import PartitionSpec as P

RMS_EPS = 1.5625e-7
ROPE_BASE = 10000.0
NEG_BIG = -3.0e38
MESH = pl.DeviceIdType.MESH
F32 = jnp.float32
BF16 = jnp.bfloat16

N_ROWS = 32
S_DEV = 512
D = 128
SP = 64
PLANE = 16
HEADS = 24
SLOT = 32
N_OUT = 6144
K_OUT = 3072
N_CUT = 1024
WO_SLOTS = 5
Q_DEV = 384
K_CUT = 1536


def step_kernel(hid_hbm, nw_hbm, bq_hbm, bk_hbm, bv_hbm, freq_ref, pos_hbm, seq_hbm,
                wq_hbm, wk_hbm, wv_hbm, k_hbm, v_hbm, wo_hbm, y_own, y_other, kn_rows, vn_rows,
                nw_ref, bq_ref, bk_ref, bv_ref, pos_ref, seq_ref, hid_ref, normed, wqbuf, wkvbuf, bq_rows, q_all,
                kbuf, vbuf, wobuf, o_send, o_recv, ag, lhs,
                vecsem, hsem, wqsem, wkvsem, q_send, q_recv,
                ksem, vsem, wsem, rs_send, rs_recv, ag_send, ag_recv, d_send, d_recv):
    c = lax.axis_index('tp')
    s = lax.axis_index('sp')
    z = lax.div(s, PLANE)
    p = lax.rem(s, PLANE)
    y_at = lax.div(p, 4)
    x_at = lax.rem(p, 4)
    qk_scale = (D ** -0.5) * math.log2(math.e)

    label = 4 * lax.rem(z, 2) + 2 * lax.rem(y_at, 2) + lax.rem(x_at, 2)
    hid_copy = pltpu.make_async_copy(hid_hbm, hid_ref, hsem)
    hid_copy.start()
    vec_copies = [pltpu.make_async_copy(src, dst, vecsem.at[j]) for j, (src, dst) in enumerate((
        (pos_hbm, pos_ref), (nw_hbm, nw_ref), (bq_hbm, bq_ref), (bk_hbm, bk_ref), (bv_hbm, bv_ref), (seq_hbm, seq_ref)))]
    for cp in vec_copies:
        cp.start()
    q_cols = pl.ds(pl.multiple_of(label * Q_DEV, D), Q_DEV)
    wq_copies = [pltpu.make_async_copy(
        wq_hbm.at[pl.ds(K_CUT * j, K_CUT), q_cols], wqbuf.at[pl.ds(K_CUT * j, K_CUT)], wqsem.at[j])
        for j in range(N_OUT // K_CUT)]
    for cp in wq_copies:
        cp.start()

    barrier = pltpu.get_barrier_semaphore()

    def greet(d, carry):
        pl.semaphore_signal(barrier, inc=1, device_id={'sp': lax.rem(s + d, SP)}, device_id_type=MESH)
        return carry
    lax.fori_loop(1, SP, greet, 0)
    pl.semaphore_signal(barrier, inc=1, device_id={'tp': 1 - c}, device_id_type=MESH)

    wkv_copies = [pltpu.make_async_copy(wk_hbm, wkvbuf.at[:, pl.ds(0, D)], wkvsem.at[0]),
                  pltpu.make_async_copy(wv_hbm, wkvbuf.at[:, pl.ds(D, D)], wkvsem.at[1])]
    for cp in wkv_copies:
        cp.start()

    own = lax.div(s, 2)
    is_owner = lax.rem(s, 2) == c

    def group_of(g):
        return lax.rem(lax.div(own, 4) + 1 + g, 8)

    def kv_copies(g):
        rows = pl.ds(4 * group_of(g), 4)
        return [pltpu.make_async_copy(k_hbm.at[rows], kbuf.at[rows], ksem.at[g]),
                pltpu.make_async_copy(v_hbm.at[rows], vbuf.at[rows], vsem.at[g])]
    wo_copies = [pltpu.make_async_copy(
        wo_hbm.at[:, pl.ds(N_CUT * j, N_CUT)], wobuf.at[j % WO_SLOTS], wsem.at[j]) for j in range(N_OUT // N_CUT)]

    vec_copies[0].wait()
    row_eye = lax.broadcasted_iota(jnp.int32, (N_ROWS, N_ROWS), 0) == lax.broadcasted_iota(jnp.int32, (N_ROWS, N_ROWS), 1)
    pos_col = jnp.sum(jnp.where(row_eye, pos_ref[...].astype(F32), 0.0), axis=1, keepdims=True)
    angles = pos_col * freq_ref[...]
    is_even = lax.rem(lax.broadcasted_iota(jnp.int32, (N_ROWS, D), 1), 2) == 0
    cos_t = jnp.cos(angles)
    sin_t = jnp.where(is_even, -jnp.sin(angles), jnp.sin(angles))

    def rotate(head):
        other = jnp.where(is_even, pltpu.roll(head, D - 1, 1), pltpu.roll(head, 1, 1))
        return (head * cos_t + other * sin_t).astype(BF16)

    hid_copy.wait()
    for cp in vec_copies[1:]:
        cp.wait()
    x_f32 = hid_ref[...].astype(F32)
    mean_sq = jnp.mean(x_f32 * x_f32, axis=-1, keepdims=True)
    unit = lax.rsqrt(mean_sq + RMS_EPS)
    nw_rows = nw_ref[...].astype(F32)
    for j in range(N_OUT // D):
        cut = slice(j * D, (j + 1) * D)
        normed[:, cut] = (x_f32[:, cut] * unit * nw_rows[j:j + 1, :]).astype(BF16)
    bq_rows[...] = bq_ref[...].astype(F32)

    q_mine = jnp.zeros((N_ROWS, Q_DEV), F32)
    for j, cp in enumerate(wq_copies):
        cp.wait()
        cut = slice(K_CUT * j, K_CUT * (j + 1))
        q_mine = q_mine + jnp.dot(normed[:, cut], wqbuf[cut, :], preferred_element_type=F32)
    for g in range(8):
        for cp in kv_copies(g):
            cp.start()

    def q_rows(lab):
        return pl.multiple_of(lab * (3 * N_ROWS), N_ROWS)
    for t in range(3):
        head = q_mine[:, t * D:(t + 1) * D] + bq_rows[pl.ds(3 * label + t, 1), :]
        q_all[pl.ds(q_rows(label) + t * N_ROWS, N_ROWS), :] = rotate(head.astype(BF16).astype(F32)).astype(F32)

    pl.semaphore_wait(barrier, SP)

    def across(v):
        return lax.rem(v + 4 + (1 - 2 * lax.rem(v, 2)) * (1 - 2 * c), 4)
    q_copies = []
    for mask in range(7, 0, -1):
        zd = across(z) if mask & 4 else z
        yd = across(y_at) if mask & 2 else y_at
        xd = across(x_at) if mask & 1 else x_at
        mine = q_all.at[pl.ds(q_rows(label), 3 * N_ROWS)]
        q_copies.append(pltpu.make_async_remote_copy(
            src_ref=mine, dst_ref=mine, send_sem=q_send.at[mask - 1], recv_sem=q_recv.at[mask - 1],
            device_id={'sp': zd * PLANE + yd * 4 + xd}, device_id_type=MESH))
    for cp in q_copies:
        cp.start()

    for cp in wkv_copies:
        cp.wait()
    kv = jnp.dot(normed[...], wkvbuf[...], preferred_element_type=F32)
    k_new = rotate((kv[:, :D] + bk_ref[...].astype(F32)).astype(BF16).astype(F32))
    v_new = (kv[:, D:] + bv_ref[...].astype(F32)).astype(BF16)
    kn_rows[...] = k_new.astype(F32)
    vn_rows[...] = v_new.astype(F32)
    for cp in q_copies:
        cp.wait_recv()

    for cp in wo_copies[:WO_SLOTS]:
        cp.start()

    eye = (lax.broadcasted_iota(jnp.int32, (HEADS, D), 0) == lax.broadcasted_iota(jnp.int32, (HEADS, D), 1))
    stat_row = lax.broadcasted_iota(jnp.int32, (SLOT - HEADS, D), 0)
    pos = s * S_DEV + lax.broadcasted_iota(jnp.int32, (HEADS, S_DEV), 1)
    mine = pl.ds(pl.multiple_of(s * SLOT, SLOT), SLOT)

    def rs_copy(b):
        return pltpu.make_async_remote_copy(
            src_ref=o_send.at[b], dst_ref=o_recv.at[mine],
            send_sem=rs_send, recv_sem=rs_recv, device_id={'sp': 2 * b + c}, device_id_type=MESH)

    def rows_step(step, carry):
        work = []
        for h in range(2):
            for cp in kv_copies(2 * step + h):
                cp.wait()
            work += [4 * group_of(2 * step + h) + lax.rem(own + 1 + u, 4) for u in range(4)]
        scores = []
        for b in work:
            sc = lax.dot_general(q_all[pl.ds(b, HEADS, stride=N_ROWS), :].astype(BF16), kbuf[b],
                                 (((1,), (1,)), ((), ())), preferred_element_type=F32)
            scores.append(jnp.where(pos < seq_ref[b], sc, NEG_BIG))
        tops = [jnp.max(sc, axis=1, keepdims=True) for sc in scores]
        probs = [jnp.exp2((sc - m) * qk_scale) for sc, m in zip(scores, tops)]
        sums = [jnp.sum(pr, axis=1, keepdims=True) for pr in probs]
        for b, m, l, pr in zip(work, tops, sums, probs):
            o_send[b, :HEADS] = jnp.dot(pr.astype(BF16), vbuf[b], preferred_element_type=F32)
            m_row = jnp.sum(jnp.where(eye, m * qk_scale, 0.0), axis=0, keepdims=True)
            l_row = jnp.sum(jnp.where(eye, l, 0.0), axis=0, keepdims=True)
            o_send[b, HEADS:] = jnp.where(stat_row == 0, m_row, l_row)
        for b in work[:-1]:
            rs_copy(b).start()

        @pl.when(2 * work[-1] + c != s)
        def _():
            rs_copy(work[-1]).start()
        return carry
    lax.fori_loop(0, 4, rows_step, 0)

    def all_in(ref, sem):
        pltpu.make_async_copy(ref, ref, sem).wait()

    def ag_copy(dz, dy, dx):
        dest = lax.rem(z + dz, 4) * PLANE + lax.rem(y_at + dy, 4) * 4 + lax.rem(x_at + dx, 4)
        slot = ag.at[pl.ds(pl.multiple_of(own * HEADS, 8), HEADS)]
        return pltpu.make_async_remote_copy(
            src_ref=slot, dst_ref=slot, send_sem=ag_send, recv_sem=ag_recv,
            device_id={'sp': dest}, device_id_type=MESH)
    far_first = sorted(((dz, dy, dx) for dz in range(4) for dy in range(4) for dx in range(4)),
                       key=lambda d: -sum(min(v, 4 - v) for v in d))[:-1]

    @pl.when(is_owner)
    def _():
        o_recv[mine, :] = o_send[own]
        k_mine = kn_rows[pl.ds(own, 1), :]
        v_mine = vn_rows[pl.ds(own, 1), :]
        s_new = jnp.sum(q_all[pl.ds(own, HEADS, stride=N_ROWS), :] * k_mine, axis=1, keepdims=True) * qk_scale
        all_in(o_recv.at[pl.ds(0, (SP - 1) * SLOT)], rs_recv)
        m_rows = o_recv[pl.ds(HEADS, SP, stride=SLOT), :]
        l_rows = o_recv[pl.ds(HEADS + 1, SP, stride=SLOT), :]
        stats = jnp.transpose(jnp.concatenate([m_rows, l_rows], axis=0))[:HEADS]
        m_cols, l_cols = stats[:, :SP], stats[:, SP:]
        m_top = jnp.maximum(jnp.max(m_cols, axis=1, keepdims=True), s_new)
        w_cols = jnp.exp2(m_cols - m_top)
        w_new = jnp.exp2(s_new - m_top)
        l_all = jnp.sum(w_cols * l_cols, axis=1, keepdims=True) + w_new
        acc = w_new * v_mine
        for j in range(SP):
            acc = acc + w_cols[:, j:j + 1] * o_recv[j * SLOT:j * SLOT + HEADS, :]
        ag[pl.ds(pl.multiple_of(own * HEADS, 8), HEADS), :] = acc / l_all
        for d in far_first:
            ag_copy(*d).start()
        all_in(ag.at[pl.ds(0, (N_ROWS - 1) * HEADS)], ag_recv)

    @pl.when(jnp.logical_not(is_owner))
    def _():
        all_in(ag, ag_recv)

    for h in range(HEADS):
        lhs[:, h * D:(h + 1) * D] = ag[pl.ds(h, N_ROWS, stride=HEADS), :].astype(BF16)

    def d_copy(j):
        return pltpu.make_async_remote_copy(
            src_ref=y_own.at[j], dst_ref=y_other.at[j], send_sem=d_send.at[j], recv_sem=d_recv.at[j],
            device_id={'tp': 1 - c}, device_id_type=MESH)

    for j in range(N_OUT // N_CUT):
        wo_copies[j].wait()
        y_own[j] = jnp.dot(lhs[...], wobuf[j % WO_SLOTS], preferred_element_type=F32)
        d_copy(j).start()
        if j + WO_SLOTS < N_OUT // N_CUT:
            wo_copies[j + WO_SLOTS].start()

    @pl.when(is_owner)
    def _():
        all_in(o_send.at[pl.ds(0, N_ROWS - 1)], rs_send)
        all_in(o_recv.at[pl.ds(0, (SP - 1) * HEADS)], ag_send)

    @pl.when(jnp.logical_not(is_owner))
    def _():
        all_in(o_send, rs_send)
    for cp in q_copies:
        cp.wait_send()
    for j in range(N_OUT // N_CUT):
        d_copy(j).wait()


def step_call(freq, *operands):
    hidden, norm_w, w_q, b_q, w_k, b_k, w_v, b_v, w_o, k_cache, v_cache, positions, seq_lens = operands
    vmem = pl.BlockSpec(memory_space=pltpu.VMEM)
    hbm = pl.BlockSpec(memory_space=pltpu.HBM)
    dma = pltpu.SemaphoreType.DMA
    return pl.pallas_call(
        step_kernel,
        out_shape=(jax.ShapeDtypeStruct((N_OUT // N_CUT, N_ROWS, N_CUT), F32),
                   jax.ShapeDtypeStruct((N_OUT // N_CUT, N_ROWS, N_CUT), F32),
                   jax.ShapeDtypeStruct((N_ROWS, D), F32), jax.ShapeDtypeStruct((N_ROWS, D), F32)),
        in_specs=[hbm, hbm, hbm, hbm, hbm, vmem, hbm, hbm, hbm, hbm, hbm, hbm, hbm, hbm],
        out_specs=(vmem,) * 4,
        scratch_shapes=[
            pltpu.VMEM((N_OUT // D, D), BF16),
            pltpu.VMEM((24, D), BF16),
            pltpu.VMEM((1, D), BF16),
            pltpu.VMEM((1, D), BF16),
            pltpu.VMEM((1, N_ROWS), jnp.int32),
            pltpu.SMEM((N_ROWS,), jnp.int32),
            pltpu.VMEM((N_ROWS, N_OUT), BF16),
            pltpu.VMEM((N_ROWS, N_OUT), BF16),
            pltpu.VMEM((N_OUT, Q_DEV), BF16),
            pltpu.VMEM((N_OUT, 2 * D), BF16),
            pltpu.VMEM((24, D), F32),
            pltpu.VMEM((HEADS * N_ROWS, D), F32),
            pltpu.VMEM((N_ROWS, S_DEV, D), BF16),
            pltpu.VMEM((N_ROWS, S_DEV, D), BF16),
            pltpu.VMEM((WO_SLOTS, K_OUT, N_CUT), BF16),
            pltpu.VMEM((N_ROWS, SLOT, D), F32),
            pltpu.VMEM((SP * SLOT, D), F32),
            pltpu.VMEM((N_ROWS * HEADS, D), F32),
            pltpu.VMEM((N_ROWS, K_OUT), BF16),
            dma((6,)), dma, dma((N_OUT // K_CUT,)), dma((2,)), dma((7,)), dma((7,)),
            dma((8,)), dma((8,)), dma((8,)), dma, dma, dma, dma, dma((N_OUT // N_CUT,)), dma((N_OUT // N_CUT,)),
        ],
        compiler_params=pltpu.CompilerParams(
            collective_id=0, has_side_effects=True, vmem_limit_bytes=52 * 1024 * 1024),
        name='decode_step',
    )(*(x if x is freq else pltpu.with_memory_space_constraint(x, pltpu.HBM) for x in (
        hidden, norm_w.reshape(-1, D), b_q.reshape(-1, D), b_k.reshape(1, -1), b_v.reshape(1, -1), freq,
        positions.reshape(1, -1), seq_lens, w_q, w_k, w_v,
        k_cache.reshape(N_ROWS, S_DEV, D), v_cache.reshape(N_ROWS, S_DEV, D), w_o)))


def finish_kernel(y_own, y_other, kn_rows, vn_rows, hid_ref, y_ref, kn_ref, vn_ref):
    kn_ref[...] = kn_rows[...].astype(BF16)
    vn_ref[...] = vn_rows[...].astype(BF16)
    for j in range(N_OUT // N_CUT):
        cut = slice(j * N_CUT, (j + 1) * N_CUT)
        y_ref[:, cut] = (hid_ref[:, cut].astype(F32) + (y_own[j] + y_other[j])).astype(BF16)


def finish(*operands):
    vmem = pl.BlockSpec(memory_space=pltpu.VMEM)
    return pl.pallas_call(
        finish_kernel,
        out_shape=(jax.ShapeDtypeStruct((N_ROWS, N_OUT), BF16),
                   jax.ShapeDtypeStruct((N_ROWS, D), BF16), jax.ShapeDtypeStruct((N_ROWS, D), BF16)),
        in_specs=[vmem] * 5, out_specs=(vmem,) * 3,
        compiler_params=pltpu.CompilerParams(vmem_limit_bytes=4 * 1024 * 1024),
        name='finish',
    )(*operands)


def solution(mesh):
    def device_step(*operands):
        lane = jnp.arange(D, dtype=jnp.int32)
        inv_freq = ROPE_BASE ** (-2.0 * (lane // 2).astype(jnp.float32) / (D // 2))
        freq = jnp.where(lane < D // 2, inv_freq, 0.0).reshape(1, D)
        y_out, k_new, v_new = finish(*step_call(freq, *operands), operands[0])
        return y_out, k_new.reshape(N_ROWS, 1, D), v_new.reshape(N_ROWS, 1, D)

    col_spec = P(None, 'tp')
    vec_spec = P('tp')
    cache_spec = P('dp', 'sp', 'tp', None)
    group_spec = P('dp', 'tp', None)
    in_specs = (P('dp', None), P(None), col_spec, vec_spec, col_spec, vec_spec, col_spec, vec_spec,
                P('tp', None), cache_spec, cache_spec, P('dp'), P('dp'))
    out_specs = (P('dp', None), group_spec, group_spec)
    return jax.shard_map(device_step, mesh=mesh, in_specs=in_specs, out_specs=out_specs, check_vma=False)
```

time: 43.1 us -> 45.3 us (1.051)
  Pallas kernels: 42.2 us -> 44.5 us
    pallas_call x1, Pallas kernels: 41.3 us -> 43.7 us  [step_call(): pl.pallas_call(step_kernel, out_shape=(jax.ShapeDtypeStruct((N_OUT // N_C...]
where the time goes in v4:
time: 45.3 us; the launch traced here: 45.2 us
  Pallas kernels  44.5 us (98%)
  between operations  0.66 us (1%)
    pallas_call x1, Pallas kernels, step_call(): pl.pallas_call(step_kernel, out_shape=(jax.ShapeDtypeStruct((N_OUT // N_C...  43.7 us

profile of v4, /device:TPU:1, one launch (start us, length us, event | category | flops | bytes accessed | tf_op | source)
XLA Modules:
  0.0 45.2 jit_solution(15811290941370620100)
XLA Ops:
  0.6 0.0 copy-start
  0.7 43.7 %decode_step.1 = (f32[6,32,1024]{2,1,0:T(8,128)S(1)}, f32[6,32,1024]{2,1,0:T(8,128)S(1)}, f32[32,128]{1,0:T(8,128)S(1)}, f32[32,128]{1,0:T(8,128)S(1)}) custom-call(bf16[32,6144]{1,0:T(8,128)(2,1)} %hid_ref.1, bf16[48,128]{1,0:T(8,128)(2,1)} %bitcast.11, bf16[24,128]{1,0:T(8,128)(2,1)} %bitcast.12, bf16[1,128]{1,0:T(2,128)(2,1)} %bitcast.13, ...), custom_call_target="tpu_custom_call" | custom-call | tf_op jit(solution)/shard_map/decode_step/pallas_call | solution.py:266
  44.4 0.0 copy-done
  44.4 0.8 %finish.1 = (bf16[32,6144]{1,0:T(8,128)(2,1)}, bf16[32,128]{1,0:T(8,128)(2,1)}, bf16[32,128]{1,0:T(8,128)(2,1)}) custom-call(f32[6,32,1024]{2,1,0:T(8,128)S(1)} %get-tuple-element.10.y_own, f32[6,32,1024]{2,1,0:T(8,128)S(1)} %get-tuple-element.11.y_other, f32[32,128]{1,0:T(8,128)S(1)} %get-tuple-element.12.kn_rows, f32[32,128]{1,0:T(8,128)S(1)} %get-tuple-element.13.vn_rows, ...), custom_call_target="tpu_custom_call" | custom-call | tf_op jit(solution)/shard_map/finish/pallas_call | solution.py:315
  (1 shorter events, 0.0 us)
Async XLA Ops:
  0.6 43.7 %copy-start = (bf16[32,6144]{1,0:T(8,128)(2,1)S(1)}, bf16[32,6144]{1,0:T(8,128)(2,1)}, u32[]{:S(2)}) copy-start(bf16[32,6144]{1,0:T(8,128)(2,1)} %hid_ref.1) | copy-start | bytes 1179652

commit v5 on v3

--- a/solution.py
+++ b/solution.py
@@ -23,7 +23,8 @@
 HALF = 12
 SLOT = 16
 N_OUT = 6144
-N_Z = 1536
+K_HALF = 1536
+N_CUT = 1024
 AG = 24
 Q_DEV = 384
 K_CUT = 1536
@@ -32,9 +33,9 @@
 def step_kernel(hid_hbm, nw_hbm, bq_hbm, bk_hbm, bv_hbm, freq_ref, pos_hbm, seq_hbm,
                 wq_hbm, wk_hbm, wv_hbm, k_hbm, v_hbm, wo_hbm, ag, kn_rows, vn_rows,
                 nw_ref, bq_ref, bk_ref, bv_ref, pos_ref, seq_ref, hid_ref, normed, wqbuf, wkvbuf, bq_rows, q_all,
-                kbuf, vbuf, wobuf, o_send, o_recv, a_all, lhs, ypart, yrecv,
+                kbuf, vbuf, wobuf, o_send, o_recv, lhs, part, others,
                 vecsem, hsem, wqsem, wkvsem, q_send, q_recv,
-                ksem, vsem, wsem, rs_send, rs_recv, z_send, z_recv, d_send, d_recv,
+                ksem, vsem, wsem, rs_send, rs_recv, x_send, x_recv,
                 ag_send, ag_recv, f_send, f_recv):
     c = lax.axis_index('tp')
     s = lax.axis_index('sp')
@@ -65,12 +66,12 @@
         return carry
     lax.fori_loop(1, SP, greet, 0)
     pl.semaphore_signal(barrier, inc=1, device_id={'tp': 1 - c}, device_id_type=MESH)
+    my_half = lax.rem(z, 2)
+    near = (z + 1 - 2 * my_half) * PLANE + p
+    pl.semaphore_signal(barrier, inc=1, device_id={'sp': near, 'tp': 1 - c}, device_id_type=MESH)
 
     wkv_copies = [pltpu.make_async_copy(wk_hbm, wkvbuf.at[:, pl.ds(0, D)], wkvsem.at[0]),
                   pltpu.make_async_copy(wv_hbm, wkvbuf.at[:, pl.ds(D, D)], wkvsem.at[1])]
-    for cp in wkv_copies:
-        cp.start()
-
     def kv_copies(step):
         y_to = lax.rem(y_at + 1 + step, 4)
         pairs = []
@@ -80,8 +81,8 @@
             pairs.append(pltpu.make_async_copy(v_hbm.at[rows], vbuf.at[rows], vsem.at[2 * step + r]))
         return pairs
     wo_copies = [pltpu.make_async_copy(
-        wo_hbm.at[pl.ds(768 * j, 768), pl.ds(pl.multiple_of(z * N_Z, N_Z), N_Z)],
-        wobuf.at[pl.ds(768 * j, 768)], wsem.at[j]) for j in range(4)]
+        wo_hbm.at[pl.ds(pl.multiple_of(my_half * K_HALF, K_HALF) + 192 * j, 192)], wobuf.at[pl.ds(192 * j, 192)],
+        wsem.at[j]) for j in range(8)]
 
     vec_copies[0].wait()
     row_eye = lax.broadcasted_iota(jnp.int32, (N_ROWS, N_ROWS), 0) == lax.broadcasted_iota(jnp.int32, (N_ROWS, N_ROWS), 1)
@@ -112,6 +113,8 @@
         cp.wait()
         cut = slice(K_CUT * j, K_CUT * (j + 1))
         q_mine = q_mine + jnp.dot(normed[:, cut], wqbuf[cut, :], preferred_element_type=F32)
+    for cp in wkv_copies:
+        cp.start()
     for step in range(4):
         for cp in kv_copies(step):
             cp.start()
@@ -127,7 +130,7 @@
         head = q_mine[:, t * D:(t + 1) * D] + bq_rows[pl.ds(3 * label + t, 1), :]
         q_all[pl.ds(q_rows(label) + t * N_ROWS, N_ROWS), :] = rotate(head.astype(BF16).astype(F32)).astype(F32)
 
-    pl.semaphore_wait(barrier, SP)
+    pl.semaphore_wait(barrier, SP + 1)
 
     def across(v):
         return lax.rem(v + 4 + (1 - 2 * lax.rem(v, 2)) * (1 - 2 * c), 4)
@@ -204,7 +207,6 @@
     o_recv[mine, :] = o_send[s]
 
     my_row = p + PLANE * lax.div(z, 2)
-    my_half = lax.rem(z, 2)
     q_own = q_all[pl.ds(my_half * SLOT * N_ROWS + my_row, SLOT, stride=N_ROWS), :]
     k_mine = kn_rows[pl.ds(my_row, 1), :]
     v_mine = vn_rows[pl.ds(my_row, 1), :]
@@ -225,98 +227,86 @@
     acc = w_new * v_mine
     for j in range(SP):
         acc = acc + w_cols[:, j:j + 1] * o_recv[j * SLOT:(j + 1) * SLOT, :]
-    a_all[z] = acc / l_all
-
-    z_copies = []
-    for dz in range(1, 4):
-        z_copies.append(pltpu.make_async_remote_copy(
-            src_ref=a_all.at[z], dst_ref=a_all.at[z], send_sem=z_send.at[dz - 1], recv_sem=z_recv.at[dz - 1],
-            device_id={'sp': lax.rem(z + dz, 4) * PLANE + p}, device_id_type=MESH))
-    for cp in z_copies:
-        cp.start()
+    attn = acc / l_all
     lhs[...] = jnp.zeros_like(lhs)
-    for cp in z_copies:
-        cp.wait_recv()
-    for zz in range(4):
-        r, hf = zz // 2, zz % 2
-        for j in range(HALF):
-            lhs[r:r + 1, (hf * HALF + j) * D:(hf * HALF + j + 1) * D] = a_all[zz, j:j + 1, :]
+    for j in range(HALF):
+        lhs[0:1, j * D:(j + 1) * D] = attn[j:j + 1, :]
     for cp in wo_copies:
         cp.wait()
-    ypart[0] = jnp.dot(lhs[...].astype(BF16), wobuf[...], preferred_element_type=F32)
-
-    d_copy = pltpu.make_async_remote_copy(
-        src_ref=ypart.at[0], dst_ref=ypart.at[1], send_sem=d_send, recv_sem=d_recv,
-        device_id={'tp': 1 - c}, device_id_type=MESH)
-    d_copy.start()
-    d_copy.wait_recv()
-    both = ypart[0] + ypart[1]
+
+    lhs_b16 = lhs[...].astype(BF16)
+    for n in range(N_OUT // N_CUT):
+        piece = jnp.dot(lhs_b16, wobuf[:, n * N_CUT:(n + 1) * N_CUT], preferred_element_type=F32)
+        half, first = n // 3, (n % 3) * (N_CUT // D)
+        for j in range(N_CUT // D):
+            row = first + j
+            part[pl.ds(lax.rem(half + my_half, 2) * AG + row, 1), :] = piece[0:1, j * D:(j + 1) * D]
+    own_part, other_part = part.at[pl.ds(0, AG)], part.at[pl.ds(AG, AG)]
+    x_copies = [
+        pltpu.make_async_remote_copy(src_ref=other_part, dst_ref=others.at[0], send_sem=x_send.at[0], recv_sem=x_recv.at[0],
+                                     device_id={'sp': near, 'tp': 1 - c}, device_id_type=MESH),
+        pltpu.make_async_remote_copy(src_ref=other_part, dst_ref=others.at[1], send_sem=x_send.at[1], recv_sem=x_recv.at[1],
+                                     device_id={'sp': near}, device_id_type=MESH),
+        pltpu.make_async_remote_copy(src_ref=own_part, dst_ref=others.at[2], send_sem=x_send.at[2], recv_sem=x_recv.at[2],
+                                     device_id={'tp': 1 - c}, device_id_type=MESH)]
+    for cp in x_copies:
+        cp.start()
+    for cp in x_copies:
+        cp.wait_recv()
 
     def ag_slot(i):
         return ag.at[pl.ds(pl.multiple_of(i * AG, 8), AG)]
-
-    for r in range(2):
-        for blk in range(12):
-            yrecv[r * 12 + blk:r * 12 + blk + 1, :] = both[r:r + 1, blk * D:(blk + 1) * D]
-    ag[pl.ds(pl.multiple_of(s * AG, 8), AG), :] = yrecv[...]
-    par = lax.rem(s + c, 2)
-
-    def ag_copy(i):
-        dest = 2 * i + par
-        return dest, pltpu.make_async_remote_copy(
-            src_ref=ag_slot(s), dst_ref=ag_slot(s), send_sem=ag_send.at[i], recv_sem=ag_recv.at[lax.div(s, 2)],
-            device_id={'sp': dest}, device_id_type=MESH)
-
-    def ag_start(i, carry):
-        dest, cp = ag_copy(i)
-
-        @pl.when(dest != s)
-        def _():
-            cp.start()
-        return carry
-    lax.fori_loop(0, SP // 2, ag_start, 0)
-
-    def forward(i):
+    ag[pl.ds(pl.multiple_of(s * AG, 8), AG), :] = (part[:AG, :] + others[2]) + (others[0] + others[1])
+
+    offsets = sorted(((dz, dy, j) for dz in range(4) for dy in range(4) for j in range(2)),
+                     key=lambda d: min(d[0], 4 - d[0]) + min(d[1], 4 - d[1]) + 1.5 * d[2])
+
+    def chip_at(dz, dy, dx):
+        return lax.rem(z + dz, 4) * PLANE + lax.rem(y_at + dy, 4) * 4 + lax.rem(x_at + dx, 4)
+
+    def ag_copy(n):
+        dz, dy, j = offsets[n]
         return pltpu.make_async_remote_copy(
-            src_ref=ag_slot(2 * i + par), dst_ref=ag_slot(2 * i + par), send_sem=f_send.at[i], recv_sem=f_recv.at[i],
-            device_id={'tp': 1 - c}, device_id_type=MESH)
-
-    def relay(i, carry):
-        src = 2 * i + par
-
-        @pl.when(src != s)
-        def _():
-            pltpu.make_async_copy(ag_slot(src), ag_slot(src), ag_recv.at[i]).wait()
-            forward(i).start()
-        return carry
-    lax.fori_loop(0, SP // 2, relay, 0)
-
-    def relayed(i, carry):
-        src = 2 * i + 1 - par
-
-        @pl.when(src != s)
-        def _():
-            pltpu.make_async_copy(ag_slot(src), ag_slot(src), f_recv.at[i]).wait()
-        return carry
-    lax.fori_loop(0, SP // 2, relayed, 0)
-
+            src_ref=ag_slot(s), dst_ref=ag_slot(s), send_sem=ag_send, recv_sem=ag_recv.at[n],
+            device_id={'sp': chip_at(dz, dy, 2 * j + c)}, device_id_type=MESH)
+
+    def forward(n):
+        dz, dy, j = offsets[n]
+        slot = ag_slot(chip_at(4 - dz, 4 - dy, 4 - 2 * j - c))
+        return slot, pltpu.make_async_remote_copy(
+            src_ref=slot, dst_ref=slot, send_sem=f_send, recv_sem=f_recv, device_id={'tp': 1 - c}, device_id_type=MESH)
+
+    def relay(n):
+        slot, cp = forward(n)
+        pltpu.make_async_copy(slot, slot, ag_recv.at[n]).wait()
+        cp.start()
+
+    for n in range(SP // 2 - 1, 0, -1):
+        ag_copy(n).start()
+
+    @pl.when(c == 1)
+    def _():
+        ag_copy(0).start()
+        relay(0)
+    for n in range(1, SP // 2):
+        relay(n)
+
+    few, many = ag.at[pl.ds(0, (SP // 2 - 1) * AG)], ag.at[pl.ds(0, SP // 2 * AG)]
+
+    @pl.when(c == 0)
+    def _():
+        all_in(many, f_recv)
+        all_in(few, f_send)
+        all_in(few, ag_send)
+
+    @pl.when(c == 1)
+    def _():
+        all_in(few, f_recv)
+        all_in(many, f_send)
+        all_in(many, ag_send)
     all_in(o_send.at[pl.ds(0, SP - 1)], rs_send)
-    for cp in q_copies + z_copies:
+    for cp in q_copies + x_copies:
         cp.wait_send()
-    d_copy.wait_send()
-
-    def drain(i, carry):
-        dest, cp = ag_copy(i)
-
-        @pl.when(dest != s)
-        def _():
-            cp.wait_send()
-
-        @pl.when(2 * i + par != s)
-        def _():
-            forward(i).wait_send()
-        return carry
-    lax.fori_loop(0, SP // 2, drain, 0)
 
 
 def step_call(freq, *operands):
@@ -345,20 +335,18 @@
             pltpu.VMEM((2 * SLOT * N_ROWS, D), F32),
             pltpu.VMEM((N_ROWS, S_DEV, D), BF16),
             pltpu.VMEM((N_ROWS, S_DEV, D), BF16),
-            pltpu.VMEM((3072, N_Z), BF16),
+            pltpu.VMEM((K_HALF, N_OUT), BF16),
             pltpu.VMEM((2 * N_ROWS, SLOT, D), F32),
             pltpu.VMEM((SP * SLOT, D), F32),
-            pltpu.VMEM((4, SLOT, D), F32),
-            pltpu.VMEM((8, 3072), F32),
-            pltpu.VMEM((2, 8, N_Z), F32),
-            pltpu.VMEM((AG, D), F32),
+            pltpu.VMEM((8, K_HALF), F32),
+            pltpu.VMEM((2 * AG, D), F32),
+            pltpu.VMEM((3, AG, D), F32),
             dma((6,)), dma, dma((N_OUT // K_CUT,)), dma((2,)), dma((7,)), dma((7,)),
-            dma((8,)), dma((8,)), dma((4,)),
-            dma, dma, dma((3,)), dma((3,)), dma, dma,
-            dma((SP // 2,)), dma((SP // 2,)), dma((SP // 2,)), dma((SP // 2,)),
+            dma((8,)), dma((8,)), dma((8,)), dma, dma, dma((3,)), dma((3,)),
+            dma, dma((SP // 2,)), dma, dma,
         ],
         compiler_params=pltpu.CompilerParams(
-            collective_id=0, has_side_effects=True, vmem_limit_bytes=36 * 1024 * 1024),
+            collective_id=0, has_side_effects=True, vmem_limit_bytes=44 * 1024 * 1024),
         name='decode_step',
     )(*(x if x is freq else pltpu.with_memory_space_constraint(x, pltpu.HBM) for x in (
         hidden, norm_w.reshape(-1, D), b_q.reshape(-1, D), b_k.reshape(1, -1), b_v.reshape(1, -1), freq,
@@ -370,12 +358,12 @@
     kn_ref[...] = kn_rows[...].astype(BF16)
     vn_ref[...] = vn_rows[...].astype(BF16)
     for zz in range(4):
-        for blk in range(12):
-            col = slice(zz * N_Z + blk * D, zz * N_Z + (blk + 1) * D)
-            for r in range(2):
-                rows = slice(PLANE * r, PLANE * (r + 1))
-                y_blk = ag[pl.ds(zz * PLANE * AG + r * 12 + blk, PLANE, stride=AG), :]
-                y_ref[rows, col] = (hid_ref[rows, col].astype(F32) + y_blk).astype(BF16)
+        r, hf = zz // 2, zz % 2
+        rows = slice(PLANE * r, PLANE * (r + 1))
+        for blk in range(AG):
+            col = slice(hf * (N_OUT // 2) + blk * D, hf * (N_OUT // 2) + (blk + 1) * D)
+            y_blk = ag[pl.ds(zz * PLANE * AG + blk, PLANE, stride=AG), :]
+            y_ref[rows, col] = (hid_ref[rows, col].astype(F32) + y_blk).astype(BF16)
 
 
 def finish(ag, kn_rows, vn_rows, hidden):

time: 43.1 us -> 47.8 us (1.11)
  Pallas kernels: 42.2 us -> 47 us
    pallas_call x1, Pallas kernels: 41.3 us -> 46.1 us  [step_call(): pl.pallas_call(step_kernel, out_shape=(jax.ShapeDtypeStruct((SP * AG, D),...]
where the time goes in v5:
time: 47.8 us; the launch traced here: 47.7 us
  Pallas kernels  47 us (98%)
  between operations  0.66 us (1%)
    pallas_call x1, Pallas kernels, step_call(): pl.pallas_call(step_kernel, out_shape=(jax.ShapeDtypeStruct((SP * AG, D),...  46.1 us

profile of v5, /device:TPU:1, one launch (start us, length us, event | category | flops | bytes accessed | tf_op | source)
XLA Modules:
  0.0 47.7 jit_solution(16775630449901827319)
XLA Ops:
  0.6 0.0 copy-start
  0.7 46.1 %decode_step.1 = (f32[1536,128]{1,0:T(8,128)S(1)}, f32[32,128]{1,0:T(8,128)S(1)}, f32[32,128]{1,0:T(8,128)S(1)}) custom-call(bf16[32,6144]{1,0:T(8,128)(2,1)} %hid_ref.1, bf16[48,128]{1,0:T(8,128)(2,1)} %bitcast.11, bf16[24,128]{1,0:T(8,128)(2,1)} %bitcast.12, bf16[1,128]{1,0:T(2,128)(2,1)} %bitcast.13, bf16[1,128]{1,0:T(2,128)(2,1)} %bitcast.14, ...), custom_call_target="tpu_custom_call" | custom-call | tf_op jit(solution)/shard_map/decode_step/pallas_call | solution.py:317
  46.8 0.0 copy-done
  46.8 0.9 %finish.1 = (bf16[32,6144]{1,0:T(8,128)(2,1)}, bf16[32,128]{1,0:T(8,128)(2,1)}, bf16[32,128]{1,0:T(8,128)(2,1)}) custom-call(f32[1536,128]{1,0:T(8,128)S(1)} %get-tuple-element.9.ag, f32[32,128]{1,0:T(8,128)S(1)} %get-tuple-element.10.kn_rows, f32[32,128]{1,0:T(8,128)S(1)} %get-tuple-element.11.vn_rows, bf16[32,6144]{1,0:T(8,128)(2,1)S(1)} %copy-done), custom_call_target="tpu_custom_call" | custom-call | tf_op jit(solution)/shard_map/finish/pallas_call | solution.py:371
  (1 shorter events, 0.0 us)
Async XLA Ops:
  0.6 46.1 %copy-start = (bf16[32,6144]{1,0:T(8,128)(2,1)S(1)}, bf16[32,6144]{1,0:T(8,128)(2,1)}, u32[]{:S(2)}) copy-start(bf16[32,6144]{1,0:T(8,128)(2,1)} %hid_ref.1) | copy-start | bytes 1179652

commit v6 on v5

--- a/solution.py
+++ b/solution.py
@@ -118,8 +118,6 @@
     for step in range(4):
         for cp in kv_copies(step):
             cp.start()
-    for cp in wo_copies:
-        cp.start()
     for hf in range(2):
         q_all[pl.ds((hf * SLOT + HALF) * N_ROWS, (SLOT - HALF) * N_ROWS), :] = jnp.zeros(((SLOT - HALF) * N_ROWS, D), F32)
 
@@ -203,6 +201,8 @@
                         rs_copy(dest).start()
         return carry
     lax.fori_loop(0, 4, rows_step, 0)
+    for cp in wo_copies:
+        cp.start()
     mine = pl.ds(pl.multiple_of(s * SLOT, SLOT), SLOT)
     o_recv[mine, :] = o_send[s]
 

time: 47.8 us -> 43.8 us (0.916)
  Pallas kernels: 47 us -> 43 us
    pallas_call x1, Pallas kernels: 46.1 us -> 42.1 us  [step_call(): pl.pallas_call(step_kernel, out_shape=(jax.ShapeDtypeStruct((SP * AG, D),...]
where the time goes in v6:
time: 43.8 us; the launch traced here: 43.7 us
  Pallas kernels  43 us (98%)
  between operations  0.66 us (2%)
    pallas_call x1, Pallas kernels, step_call(): pl.pallas_call(step_kernel, out_shape=(jax.ShapeDtypeStruct((SP * AG, D),...  42.1 us
    pallas_call x1, Pallas kernels, finish(): pl.pallas_call(finish_kernel, out_shape=(jax.ShapeDtypeStruct((N_ROWS, N_...  0.92 us

profile of v6, /device:TPU:1, one launch (start us, length us, event | category | flops | bytes accessed | tf_op | source)
XLA Modules:
  0.0 43.7 jit_solution(9756368826042046924)
XLA Ops:
  0.6 0.0 copy-start
  0.7 42.1 %decode_step.1 = (f32[1536,128]{1,0:T(8,128)S(1)}, f32[32,128]{1,0:T(8,128)S(1)}, f32[32,128]{1,0:T(8,128)S(1)}) custom-call(bf16[32,6144]{1,0:T(8,128)(2,1)} %hid_ref.1, bf16[48,128]{1,0:T(8,128)(2,1)} %bitcast.11, bf16[24,128]{1,0:T(8,128)(2,1)} %bitcast.12, bf16[1,128]{1,0:T(2,128)(2,1)} %bitcast.13, bf16[1,128]{1,0:T(2,128)(2,1)} %bitcast.14, ...), custom_call_target="tpu_custom_call" | custom-call | tf_op jit(solution)/shard_map/decode_step/pallas_call | solution.py:317
  42.8 0.0 copy-done
  42.8 0.9 %finish.1 = (bf16[32,6144]{1,0:T(8,128)(2,1)}, bf16[32,128]{1,0:T(8,128)(2,1)}, bf16[32,128]{1,0:T(8,128)(2,1)}) custom-call(f32[1536,128]{1,0:T(8,128)S(1)} %get-tuple-element.9.ag, f32[32,128]{1,0:T(8,128)S(1)} %get-tuple-element.10.kn_rows, f32[32,128]{1,0:T(8,128)S(1)} %get-tuple-element.11.vn_rows, bf16[32,6144]{1,0:T(8,128)(2,1)S(1)} %copy-done), custom_call_target="tpu_custom_call" | custom-call | tf_op jit(solution)/shard_map/finish/pallas_call | solution.py:371
  (1 shorter events, 0.0 us)
Async XLA Ops:
  0.6 42.1 %copy-start = (bf16[32,6144]{1,0:T(8,128)(2,1)S(1)}, bf16[32,6144]{1,0:T(8,128)(2,1)}, u32[]{:S(2)}) copy-start(bf16[32,6144]{1,0:T(8,128)(2,1)} %hid_ref.1) | copy-start | bytes 1179652

commit v7 on v6

--- a/solution.py
+++ b/solution.py
@@ -151,6 +151,11 @@
     v_new = (kv[:, D:] + bv_ref[...].astype(F32)).astype(BF16)
     kn_rows[...] = k_new.astype(F32)
     vn_rows[...] = v_new.astype(F32)
+    for step in range(4):
+        for cp in kv_copies(step):
+            cp.wait()
+    for cp in wo_copies:
+        cp.start()
     for cp in q_copies:
         cp.wait_recv()
 
@@ -166,8 +171,6 @@
 
     def rows_step(step, carry):
         y_to = lax.rem(y_at + 1 + step, 4)
-        for cp in kv_copies(step):
-            cp.wait()
         work = []
         for u in range(4):
             for r in range(2):
@@ -201,8 +204,6 @@
                         rs_copy(dest).start()
         return carry
     lax.fori_loop(0, 4, rows_step, 0)
-    for cp in wo_copies:
-        cp.start()
     mine = pl.ds(pl.multiple_of(s * SLOT, SLOT), SLOT)
     o_recv[mine, :] = o_send[s]
 
@@ -235,28 +236,30 @@
         cp.wait()
 
     lhs_b16 = lhs[...].astype(BF16)
-    for n in range(N_OUT // N_CUT):
-        piece = jnp.dot(lhs_b16, wobuf[:, n * N_CUT:(n + 1) * N_CUT], preferred_element_type=F32)
-        half, first = n // 3, (n % 3) * (N_CUT // D)
-        for j in range(N_CUT // D):
-            row = first + j
-            part[pl.ds(lax.rem(half + my_half, 2) * AG + row, 1), :] = piece[0:1, j * D:(j + 1) * D]
-    own_part, other_part = part.at[pl.ds(0, AG)], part.at[pl.ds(AG, AG)]
-    x_copies = [
-        pltpu.make_async_remote_copy(src_ref=other_part, dst_ref=others.at[0], send_sem=x_send.at[0], recv_sem=x_recv.at[0],
-                                     device_id={'sp': near, 'tp': 1 - c}, device_id_type=MESH),
-        pltpu.make_async_remote_copy(src_ref=other_part, dst_ref=others.at[1], send_sem=x_send.at[1], recv_sem=x_recv.at[1],
-                                     device_id={'sp': near}, device_id_type=MESH),
-        pltpu.make_async_remote_copy(src_ref=own_part, dst_ref=others.at[2], send_sem=x_send.at[2], recv_sem=x_recv.at[2],
-                                     device_id={'tp': 1 - c}, device_id_type=MESH)]
-    for cp in x_copies:
-        cp.start()
+
+    def product(half, place):
+        for n in range(N_OUT // 2 // N_CUT):
+            cols = pl.ds(pl.multiple_of(half * (N_OUT // 2) + n * N_CUT, N_CUT), N_CUT)
+            piece = jnp.dot(lhs_b16, wobuf[:, cols], preferred_element_type=F32)
+            for j in range(N_CUT // D):
+                part[place, n * (N_CUT // D) + j:n * (N_CUT // D) + j + 1, :] = piece[0:1, j * D:(j + 1) * D]
+
+    def x_copy(n, place, target):
+        return pltpu.make_async_remote_copy(
+            src_ref=part.at[place], dst_ref=others.at[n], send_sem=x_send.at[n], recv_sem=x_recv.at[n],
+            device_id=target, device_id_type=MESH)
+    x_copies = [x_copy(0, 1, {'sp': near, 'tp': 1 - c}), x_copy(1, 1, {'sp': near}), x_copy(2, 0, {'tp': 1 - c})]
+    product(1 - my_half, 1)
+    x_copies[0].start()
+    x_copies[1].start()
+    product(my_half, 0)
+    x_copies[2].start()
     for cp in x_copies:
         cp.wait_recv()
 
     def ag_slot(i):
         return ag.at[pl.ds(pl.multiple_of(i * AG, 8), AG)]
-    ag[pl.ds(pl.multiple_of(s * AG, 8), AG), :] = (part[:AG, :] + others[2]) + (others[0] + others[1])
+    ag[pl.ds(pl.multiple_of(s * AG, 8), AG), :] = (part[0] + others[2]) + (others[0] + others[1])
 
     offsets = sorted(((dz, dy, j) for dz in range(4) for dy in range(4) for j in range(2)),
                      key=lambda d: min(d[0], 4 - d[0]) + min(d[1], 4 - d[1]) + 1.5 * d[2])
@@ -281,12 +284,22 @@
         pltpu.make_async_copy(slot, slot, ag_recv.at[n]).wait()
         cp.start()
 
-    for n in range(SP // 2 - 1, 0, -1):
-        ag_copy(n).start()
+    def to_first_row(n):
+        dz, dy, j = offsets[n]
+        return jnp.logical_and(lax.rem(z + dz, 4) == 0, lax.rem(y_at + dy, 4) == 0)
+
+    def ag_starts(wanted):
+        for n in range(SP // 2 - 1, -1, -1):
+            go = wanted(n) if n else jnp.logical_and(wanted(n), c == 1)
+
+            @pl.when(go)
+            def _():
+                ag_copy(n).start()
+    ag_starts(to_first_row)
+    ag_starts(lambda n: jnp.logical_not(to_first_row(n)))
 
     @pl.when(c == 1)
     def _():
-        ag_copy(0).start()
         relay(0)
     for n in range(1, SP // 2):
         relay(n)
@@ -339,7 +352,7 @@
             pltpu.VMEM((2 * N_ROWS, SLOT, D), F32),
             pltpu.VMEM((SP * SLOT, D), F32),
             pltpu.VMEM((8, K_HALF), F32),
-            pltpu.VMEM((2 * AG, D), F32),
+            pltpu.VMEM((2, AG, D), F32),
             pltpu.VMEM((3, AG, D), F32),
             dma((6,)), dma, dma((N_OUT // K_CUT,)), dma((2,)), dma((7,)), dma((7,)),
             dma((8,)), dma((8,)), dma((8,)), dma, dma, dma((3,)), dma((3,)),

time: 43.8 us -> 41.8 us (0.954)
  Pallas kernels: 43 us -> 41 us
    pallas_call x1, Pallas kernels: 42.1 us -> 40.1 us  [step_call(): pl.pallas_call(step_kernel, out_shape=(jax.ShapeDtypeStruct((SP * AG, D),...]
where the time goes in v7:
time: 41.8 us; the launch traced here: 41.7 us
  Pallas kernels  41 us (98%)
  between operations  0.66 us (2%)
    pallas_call x1, Pallas kernels, step_call(): pl.pallas_call(step_kernel, out_shape=(jax.ShapeDtypeStruct((SP * AG, D),...  40.1 us
    pallas_call x1, Pallas kernels, finish(): pl.pallas_call(finish_kernel, out_shape=(jax.ShapeDtypeStruct((N_ROWS, N_...  0.92 us

profile of v7, /device:TPU:1, one launch (start us, length us, event | category | flops | bytes accessed | tf_op | source)
XLA Modules:
  0.0 41.7 jit_solution(10935850943597768195)
XLA Ops:
  0.6 0.0 copy-start
  0.7 40.1 %decode_step.1 = (f32[1536,128]{1,0:T(8,128)S(1)}, f32[32,128]{1,0:T(8,128)S(1)}, f32[32,128]{1,0:T(8,128)S(1)}) custom-call(bf16[32,6144]{1,0:T(8,128)(2,1)} %hid_ref.1, bf16[48,128]{1,0:T(8,128)(2,1)} %bitcast.11, bf16[24,128]{1,0:T(8,128)(2,1)} %bitcast.12, bf16[1,128]{1,0:T(2,128)(2,1)} %bitcast.13, bf16[1,128]{1,0:T(2,128)(2,1)} %bitcast.14, ...), custom_call_target="tpu_custom_call" | custom-call | tf_op jit(solution)/shard_map/decode_step/pallas_call | solution.py:330
  40.8 0.0 copy-done
  40.8 0.9 %finish.1 = (bf16[32,6144]{1,0:T(8,128)(2,1)}, bf16[32,128]{1,0:T(8,128)(2,1)}, bf16[32,128]{1,0:T(8,128)(2,1)}) custom-call(f32[1536,128]{1,0:T(8,128)S(1)} %get-tuple-element.9.ag, f32[32,128]{1,0:T(8,128)S(1)} %get-tuple-element.10.kn_rows, f32[32,128]{1,0:T(8,128)S(1)} %get-tuple-element.11.vn_rows, bf16[32,6144]{1,0:T(8,128)(2,1)S(1)} %copy-done), custom_call_target="tpu_custom_call" | custom-call | tf_op jit(solution)/shard_map/finish/pallas_call | solution.py:384
  (1 shorter events, 0.0 us)
Async XLA Ops:
  0.6 40.1 %copy-start = (bf16[32,6144]{1,0:T(8,128)(2,1)S(1)}, bf16[32,6144]{1,0:T(8,128)(2,1)}, u32[]{:S(2)}) copy-start(bf16[32,6144]{1,0:T(8,128)(2,1)} %hid_ref.1) | copy-start | bytes 1179652

commit v8 on v7

--- a/solution.py
+++ b/solution.py
@@ -45,6 +45,21 @@
     x_at = lax.rem(p, 4)
     qk_scale = (D ** -0.5) * math.log2(math.e)
 
+    def chip_at(dz, dy, dx):
+        return lax.rem(z + dz, 4) * PLANE + lax.rem(y_at + dy, 4) * 4 + lax.rem(x_at + dx, 4)
+
+    barrier = pltpu.get_barrier_semaphore()
+    far_first = sorted(((dz, dy, dx) for dz in range(4) for dy in range(4) for dx in range(4)),
+                       key=lambda d: -sum(min(v, 4 - v) for v in d))[:-1]
+    for dz, dy, dx in far_first:
+        pl.semaphore_signal(barrier, inc=1, device_id={'sp': chip_at(dz, dy, dx)}, device_id_type=MESH)
+    pl.semaphore_signal(barrier, inc=1, device_id={'tp': 1 - c}, device_id_type=MESH)
+    my_half = lax.rem(z, 2)
+    near = (z + 1 - 2 * my_half) * PLANE + p
+    pl.semaphore_signal(barrier, inc=1, device_id={'sp': near, 'tp': 1 - c}, device_id_type=MESH)
+
+    wkv_copies = [pltpu.make_async_copy(wk_hbm, wkvbuf.at[:, pl.ds(0, D)], wkvsem.at[0]),
+                  pltpu.make_async_copy(wv_hbm, wkvbuf.at[:, pl.ds(D, D)], wkvsem.at[1])]
     label = 4 * lax.rem(z, 2) + 2 * lax.rem(y_at, 2) + lax.rem(x_at, 2)
     hid_copy = pltpu.make_async_copy(hid_hbm, hid_ref, hsem)
     hid_copy.start()
@@ -59,19 +74,6 @@
     for cp in wq_copies:
         cp.start()
 
-    barrier = pltpu.get_barrier_semaphore()
-
-    def greet(d, carry):
-        pl.semaphore_signal(barrier, inc=1, device_id={'sp': lax.rem(s + d, SP)}, device_id_type=MESH)
-        return carry
-    lax.fori_loop(1, SP, greet, 0)
-    pl.semaphore_signal(barrier, inc=1, device_id={'tp': 1 - c}, device_id_type=MESH)
-    my_half = lax.rem(z, 2)
-    near = (z + 1 - 2 * my_half) * PLANE + p
-    pl.semaphore_signal(barrier, inc=1, device_id={'sp': near, 'tp': 1 - c}, device_id_type=MESH)
-
-    wkv_copies = [pltpu.make_async_copy(wk_hbm, wkvbuf.at[:, pl.ds(0, D)], wkvsem.at[0]),
-                  pltpu.make_async_copy(wv_hbm, wkvbuf.at[:, pl.ds(D, D)], wkvsem.at[1])]
     def kv_copies(step):
         y_to = lax.rem(y_at + 1 + step, 4)
         pairs = []
@@ -263,9 +265,6 @@
 
     offsets = sorted(((dz, dy, j) for dz in range(4) for dy in range(4) for j in range(2)),
                      key=lambda d: min(d[0], 4 - d[0]) + min(d[1], 4 - d[1]) + 1.5 * d[2])
-
-    def chip_at(dz, dy, dx):
-        return lax.rem(z + dz, 4) * PLANE + lax.rem(y_at + dy, 4) * 4 + lax.rem(x_at + dx, 4)
 
     def ag_copy(n):
         dz, dy, j = offsets[n]
@@ -367,9 +366,10 @@
         k_cache.reshape(N_ROWS, S_DEV, D), v_cache.reshape(N_ROWS, S_DEV, D), w_o)))
 
 
-def finish_kernel(ag, kn_rows, vn_rows, hid_ref, y_ref, kn_ref, vn_ref):
+def finish_kernel(ag, kn_rows, vn_rows, hid_ref, y_hbm, kn_hbm, vn_hbm, y_ref, kn_ref, vn_ref, sems):
     kn_ref[...] = kn_rows[...].astype(BF16)
     vn_ref[...] = vn_rows[...].astype(BF16)
+    copies = [pltpu.make_async_copy(kn_ref, kn_hbm, sems.at[0]), pltpu.make_async_copy(vn_ref, vn_hbm, sems.at[1])]
     for zz in range(4):
         r, hf = zz // 2, zz % 2
         rows = slice(PLANE * r, PLANE * (r + 1))
@@ -377,15 +377,26 @@
             col = slice(hf * (N_OUT // 2) + blk * D, hf * (N_OUT // 2) + (blk + 1) * D)
             y_blk = ag[pl.ds(zz * PLANE * AG + blk, PLANE, stride=AG), :]
             y_ref[rows, col] = (hid_ref[rows, col].astype(F32) + y_blk).astype(BF16)
+        block = (pl.ds(PLANE * r, PLANE), pl.ds(hf * (N_OUT // 2), N_OUT // 2))
+        copies.append(pltpu.make_async_copy(y_ref.at[block], y_hbm.at[block], sems.at[2 + zz]))
+        if zz == 0:
+            copies[0].start()
+            copies[1].start()
+        copies[-1].start()
+    for cp in copies:
+        cp.wait()
 
 
 def finish(ag, kn_rows, vn_rows, hidden):
     vmem = pl.BlockSpec(memory_space=pltpu.VMEM)
+    hbm = pl.BlockSpec(memory_space=pltpu.HBM)
     return pl.pallas_call(
         finish_kernel,
         out_shape=(jax.ShapeDtypeStruct((N_ROWS, N_OUT), BF16),
                    jax.ShapeDtypeStruct((N_ROWS, D), BF16), jax.ShapeDtypeStruct((N_ROWS, D), BF16)),
-        in_specs=[vmem] * 4, out_specs=(vmem,) * 3,
+        in_specs=[vmem] * 4, out_specs=(hbm,) * 3,
+        scratch_shapes=[pltpu.VMEM((N_ROWS, N_OUT), BF16), pltpu.VMEM((N_ROWS, D), BF16),
+                        pltpu.VMEM((N_ROWS, D), BF16), pltpu.SemaphoreType.DMA((6,))],
         compiler_params=pltpu.CompilerParams(vmem_limit_bytes=8 * 1024 * 1024),
         name='finish',
     )(ag, kn_rows, vn_rows, hidden)

time: 41.8 us -> 41.2 us (0.986)
  Pallas kernels: 41 us -> 40.4 us
    pallas_call x1, Pallas kernels: 40.1 us -> 39.5 us  [step_call(): pl.pallas_call(step_kernel, out_shape=(jax.ShapeDtypeStruct((SP * AG, D),...]
where the time goes in v8:
time: 41.2 us; the launch traced here: 41 us
  Pallas kernels  40.4 us (98%)
  between operations  0.66 us (2%)
    pallas_call x1, Pallas kernels, step_call(): pl.pallas_call(step_kernel, out_shape=(jax.ShapeDtypeStruct((SP * AG, D),...  39.5 us
    pallas_call x1, Pallas kernels, finish(): pl.pallas_call(finish_kernel, out_shape=(jax.ShapeDtypeStruct((N_ROWS, N_...  0.86 us

profile of v8, /device:TPU:1, one launch (start us, length us, event | category | flops | bytes accessed | tf_op | source)
XLA Modules:
  0.0 41.0 jit_solution(11482332252651975248)
XLA Ops:
  0.6 0.0 copy-start
  0.7 39.5 %decode_step.1 = (f32[1536,128]{1,0:T(8,128)S(1)}, f32[32,128]{1,0:T(8,128)S(1)}, f32[32,128]{1,0:T(8,128)S(1)}) custom-call(bf16[32,6144]{1,0:T(8,128)(2,1)} %hid_ref.1, bf16[48,128]{1,0:T(8,128)(2,1)} %bitcast.11, bf16[24,128]{1,0:T(8,128)(2,1)} %bitcast.12, bf16[1,128]{1,0:T(2,128)(2,1)} %bitcast.13, bf16[1,128]{1,0:T(2,128)(2,1)} %bitcast.14, ...), custom_call_target="tpu_custom_call" | custom-call | tf_op jit(solution)/shard_map/decode_step/pallas_call | solution.py:329
  40.2 0.0 copy-done
  40.2 0.9 %finish.1 = (bf16[32,6144]{1,0:T(8,128)(2,1)}, bf16[32,128]{1,0:T(8,128)(2,1)}, bf16[32,128]{1,0:T(8,128)(2,1)}) custom-call(f32[1536,128]{1,0:T(8,128)S(1)} %get-tuple-element.9.ag, f32[32,128]{1,0:T(8,128)S(1)} %get-tuple-element.10.kn_rows, f32[32,128]{1,0:T(8,128)S(1)} %get-tuple-element.11.vn_rows, bf16[32,6144]{1,0:T(8,128)(2,1)S(1)} %copy-done), custom_call_target="tpu_custom_call" | custom-call | tf_op jit(solution)/shard_map/finish/pallas_call | solution.py:393
  (1 shorter events, 0.0 us)
Async XLA Ops:
  0.6 39.5 %copy-start = (bf16[32,6144]{1,0:T(8,128)(2,1)S(1)}, bf16[32,6144]{1,0:T(8,128)(2,1)}, u32[]{:S(2)}) copy-start(bf16[32,6144]{1,0:T(8,128)(2,1)} %hid_ref.1) | copy-start | bytes 1179652

commit v9 on v8

--- a/solution.py
+++ b/solution.py
@@ -74,8 +74,11 @@
     for cp in wq_copies:
         cp.start()
 
+    def far_rows(step):
+        return jnp.where(step == 0, 2, jnp.where(step == 1, 1, jnp.where(step == 2, 3, 0)))
+
     def kv_copies(step):
-        y_to = lax.rem(y_at + 1 + step, 4)
+        y_to = lax.rem(y_at + far_rows(step), 4)
         pairs = []
         for r in range(2):
             rows = pl.ds(PLANE * r + 4 * y_to, 4)
@@ -172,11 +175,11 @@
             send_sem=rs_send, recv_sem=rs_recv, device_id={'sp': dest}, device_id_type=MESH)
 
     def rows_step(step, carry):
-        y_to = lax.rem(y_at + 1 + step, 4)
+        y_to = lax.rem(y_at + far_rows(step), 4)
         work = []
         for u in range(4):
             for r in range(2):
-                chip = 4 * y_to + lax.rem(x_at + 1 + u, 4)
+                chip = 4 * y_to + lax.rem(x_at + (2, 1, 3, 0)[u], 4)
                 work.append((u, r, chip, chip + PLANE * r))
         scores = []
         for u, r, chip, b in work:
@@ -186,24 +189,26 @@
         tops = [jnp.max(sc, axis=1, keepdims=True) for sc in scores]
         probs = [jnp.exp2((sc - m) * qk_scale) for sc, m in zip(scores, tops)]
         sums = [jnp.sum(pr, axis=1, keepdims=True) for pr in probs]
-        for (u, r, chip, b), m, l, pr in zip(work, tops, sums, probs):
-            o = jnp.dot(pr.astype(BF16), vbuf[b], preferred_element_type=F32)
-            m2 = m * qk_scale
-            for hf in range(2):
-                part = slice(hf * SLOT, (hf + 1) * SLOT)
-                m_row = jnp.sum(jnp.where(eye, m2[part], 0.0), axis=0, keepdims=True)
-                l_row = jnp.sum(jnp.where(eye, l[part], 0.0), axis=0, keepdims=True)
-                o_send[(2 * r + hf) * PLANE + chip] = jnp.where(
-                    sub == HALF, m_row, jnp.where(sub == HALF + 1, l_row, o[part]))
-        for u, r, chip, b in work:
-            for hf in range(2):
-                dest = (2 * r + hf) * PLANE + chip
-                if u < 3:
-                    rs_copy(dest).start()
-                else:
-                    @pl.when(dest != s)
-                    def _():
+        parts = list(zip(work, tops, sums, probs))
+        for group in (parts[:4], parts[4:]):
+            for (u, r, chip, b), m, l, pr in group:
+                o = jnp.dot(pr.astype(BF16), vbuf[b], preferred_element_type=F32)
+                m2 = m * qk_scale
+                for hf in range(2):
+                    part = slice(hf * SLOT, (hf + 1) * SLOT)
+                    m_row = jnp.sum(jnp.where(eye, m2[part], 0.0), axis=0, keepdims=True)
+                    l_row = jnp.sum(jnp.where(eye, l[part], 0.0), axis=0, keepdims=True)
+                    o_send[(2 * r + hf) * PLANE + chip] = jnp.where(
+                        sub == HALF, m_row, jnp.where(sub == HALF + 1, l_row, o[part]))
+            for (u, r, chip, b), m, l, pr in group:
+                for hf in range(2):
+                    dest = (2 * r + hf) * PLANE + chip
+                    if u < 3:
                         rs_copy(dest).start()
+                    else:
+                        @pl.when(dest != s)
+                        def _():
+                            rs_copy(dest).start()
         return carry
     lax.fori_loop(0, 4, rows_step, 0)
     mine = pl.ds(pl.multiple_of(s * SLOT, SLOT), SLOT)

time: 41.2 us -> 40.9 us (level)
  no operation moved by 1% of the time
where the time goes in v9:
time: 40.9 us; the launch traced here: 40.8 us
  Pallas kernels  40.1 us (98%)
  between operations  0.66 us (2%)
    pallas_call x1, Pallas kernels, step_call(): pl.pallas_call(step_kernel, out_shape=(jax.ShapeDtypeStruct((SP * AG, D),...  39.3 us
    pallas_call x1, Pallas kernels, finish(): pl.pallas_call(finish_kernel, out_shape=(jax.ShapeDtypeStruct((N_ROWS, N_...  0.86 us

profile of v9, /device:TPU:1, one launch (start us, length us, event | category | flops | bytes accessed | tf_op | source)
XLA Modules:
  0.0 40.8 jit_solution(8796358636369233361)
XLA Ops:
  0.6 0.0 copy-start
  0.7 39.3 %decode_step.1 = (f32[1536,128]{1,0:T(8,128)S(1)}, f32[32,128]{1,0:T(8,128)S(1)}, f32[32,128]{1,0:T(8,128)S(1)}) custom-call(bf16[32,6144]{1,0:T(8,128)(2,1)} %hid_ref.1, bf16[48,128]{1,0:T(8,128)(2,1)} %bitcast.11, bf16[24,128]{1,0:T(8,128)(2,1)} %bitcast.12, bf16[1,128]{1,0:T(2,128)(2,1)} %bitcast.13, bf16[1,128]{1,0:T(2,128)(2,1)} %bitcast.14, ...), custom_call_target="tpu_custom_call" | custom-call | tf_op jit(solution)/shard_map/decode_step/pallas_call | solution.py:334
  39.9 0.0 copy-done
  39.9 0.9 %finish.1 = (bf16[32,6144]{1,0:T(8,128)(2,1)}, bf16[32,128]{1,0:T(8,128)(2,1)}, bf16[32,128]{1,0:T(8,128)(2,1)}) custom-call(f32[1536,128]{1,0:T(8,128)S(1)} %get-tuple-element.9.ag, f32[32,128]{1,0:T(8,128)S(1)} %get-tuple-element.10.kn_rows, f32[32,128]{1,0:T(8,128)S(1)} %get-tuple-element.11.vn_rows, bf16[32,6144]{1,0:T(8,128)(2,1)S(1)} %copy-done), custom_call_target="tpu_custom_call" | custom-call | tf_op jit(solution)/shard_map/finish/pallas_call | solution.py:398
  (1 shorter events, 0.0 us)
Async XLA Ops:
  0.6 39.3 %copy-start = (bf16[32,6144]{1,0:T(8,128)(2,1)S(1)}, bf16[32,6144]{1,0:T(8,128)(2,1)}, u32[]{:S(2)}) copy-start(bf16[32,6144]{1,0:T(8,128)(2,1)} %hid_ref.1) | copy-start | bytes 1179652
